TPU v7x, 256 devices: a whole 4x4x8 slice. The times are simulated.
256 devices in a mesh: pb: 8 (over x, core), pq: 32 (over z, y).
Axes of the slice: x: 4, y: 4, z: 8, core: 2. Of those that a mesh axis runs over, the one named last changes fastest.
Arguments:
- chol_vv: bfloat16 [352, 1792, 1792], P('pb', 'pq'), may hold values from -6 to 6
- chol_ov: bfloat16 [352, 256, 1792], P('pb', 'pq'), may hold values from -6 to 6
- chol_oo: bfloat16 [352, 256, 256], P('pb', 'pq'), may hold values from -6 to 6
- chol_vo: bfloat16 [352, 256, 1792], P('pb', None, 'pq'), may hold values from -6 to 6
- amplitudes: bfloat16 [256, 1792], P(None, 'pq'), may hold values from -0.125 to 0.125
Outputs:
- dressed: bfloat16 [352, 256, 1792], P('pb', 'pq')
- fock_ov: float32 [256, 1792], P('pq')
All inputs are finite; a program needn't handle non-finite values.
Results may differ from a plain program's by a relative error of at most 0.0081.
Values may be sent and summed in bfloat16 or wider, within the bound.
No kernel may reach another device: no remote copies, remote signals or barrier semaphores. Data moves between devices by JAX's collectives and lax.ppermute only.
A program may use at most 64 MiB of HBM per device.

v0:
```python
import jax
import jax.numpy as jnp
from jax import lax
from jax.sharding import PartitionSpec as P


def laid_out(blocks, dim):
    dims = list(blocks.shape[1:])
    dims[dim] *= blocks.shape[0]
    return jnp.moveaxis(blocks, 0, dim).reshape(dims)


def copy_for_each(shard, axis):
    copies = jnp.broadcast_to(shard, (lax.axis_size(axis), *shard.shape))
    return lax.all_to_all(copies, axis, split_axis=0, concat_axis=0, tiled=True)


def gathered_copies(shard, axis, dim):
    return laid_out(copy_for_each(shard, axis), dim)


def taken_together(shard, axis):
    everything = copy_for_each(shard, axis)
    return jnp.sum(everything, axis=0)


def per_device(chol_vv, chol_ov, chol_oo, chol_vo, amplitudes):
    batch = chol_vv.shape[0]
    occ_rows = chol_ov.shape[1]
    whole_amps = gathered_copies(amplitudes, "pq", 1)
    lprime = (
        chol_oo.astype(jnp.float32)
        + jnp.einsum("qjb,ib->qji", chol_ov, whole_amps, preferred_element_type=jnp.float32)
    ).astype(jnp.bfloat16)
    direct = jnp.einsum("qab,ib->qia", chol_vv, whole_amps, preferred_element_type=jnp.float32)
    partial_sum = chol_vo.astype(jnp.float32) + direct
    moved_sum = lax.all_to_all(
        partial_sum.astype(jnp.bfloat16), "pq", split_axis=1, concat_axis=2, tiled=True
    ).astype(partial_sum.dtype)
    moved_lprime = lax.all_to_all(lprime, "pq", split_axis=2, concat_axis=1, tiled=True)
    occupied = jnp.einsum(
        "qji,ja->qia", moved_lprime, whole_amps, preferred_element_type=jnp.float32
    )
    dressed = (moved_sum - occupied).astype(jnp.bfloat16)
    row_start = lax.axis_index("pq") * occ_rows
    own_amps = lax.dynamic_slice_in_dim(whole_amps, row_start, occ_rows, 0)
    local_coulomb = 2.0 * jnp.einsum(
        "qia,ia->q", dressed, own_amps, preferred_element_type=jnp.float32
    )
    coulomb = taken_together(local_coulomb, "pq")
    local_fock = jnp.sum(coulomb[:, None, None] * dressed.astype(jnp.float32), axis=0)
    fock_ov = taken_together(local_fock, "pb") / (batch * lax.axis_size("pb"))
    return (dressed, fock_ov)


def solution(mesh):
    in_specs = (
        P("pb", "pq", None),
        P("pb", "pq", None),
        P("pb", "pq", None),
        P("pb", None, "pq"),
        P(None, "pq"),
    )
    out_specs = (P("pb", "pq", None), P("pq", None))
    return jax.shard_map(
        per_device, mesh=mesh, in_specs=in_specs, out_specs=out_specs, check_vma=False
    )
```

profile of v0, /device:TPU:1, one launch (start us, length us, event | category | flops | bytes accessed | tf_op | source)
XLA Modules:
  0.0 155.8 jit_solution(2458996371990854179)
XLA Ops:
  0.6 0.0 copy-start
  0.6 0.0 copy-start.2
  0.7 0.9 broadcast_in_dim.10
  1.6 35.4 %all_to_all.43 = bf16[32,256,56]{1,2,0:T(8,128)(2,1)S(1)} all-to-all(bf16[32,256,56]{1,2,0:T(8,128)(2,1)S(1)} %broadcast_in_dim.10), channel_id=1, replica_groups=mesh['pb'=8,'pq'=32] {'pq'}, dimensions={0} | all-to-all | bytes 1835008 | tf_op jit(solution)/shard_map/all_to_all | solution.py:15
  37.0 0.0 copy-done
  37.0 0.0 copy-done.2
  37.0 0.5 fusion.4
  37.5 0.4 copy.53
  37.9 1.9 %reshape.26 = bf16[32,2,1408]{2,1,0:T(2,128)(2,1)} reshape(bf16[256,8,44]{2,1,0:T(8,128)(2,1)S(1)} %bitcast.46) | data formatting | bytes 360448
  39.8 6.1 %all-to-all-start.2 = ((bf16[32,2,1408]{2,1,0:T(2,128)(2,1)}), bf16[32,2,1408]{2,1,0:T(2,128)(2,1)}, u32[]{:S(2)}, u32[]{:S(2)}) async-start(bf16[32,2,1408]{2,1,0:T(2,128)(2,1)} %reshape.26), calls=%async_computation.2 | async-start | bytes 360448 | tf_op jit(solution)/shard_map/all_to_all | solution.py:40
  45.9 6.3 %fusion.1 = bf16[44,256,56]{1,2,0:T(8,128)(2,1)S(1)} fusion(bf16[44,256,56]{1,2,0:T(8,128)(2,1)} %param.8, bf16[256,1792,1]{0,1,2:T(8,128)(2,1)S(1)} %bitcast.43, bf16[44,56,1792]{2,1,0:T(8,128)(2,1)} %param.5), kind=kOutput, calls=%fused_computation.4 | convolution fusion | flops 2262622208 | bytes 12271616 | tf_op jit(solution)/shard_map/qab,ib->qia/dot_general | solution.py:35
  52.2 4.5 %copy.49 = bf16[44,256,56]{2,0,1:T(8,128)(2,1)} copy(bf16[44,256,56]{1,2,0:T(8,128)(2,1)S(1)} %fusion.1) | data formatting | bytes 2523136 | tf_op jit(solution)/shard_map/convert_element_type | solution.py:38
  56.7 6.4 %reshape.24 = bf16[32,2,9856]{2,1,0:T(2,128)(2,1)} reshape(bf16[256,44,56]{2,1,0:T(8,128)(2,1)} %bitcast.41) | data formatting | bytes 2523136
  63.1 0.0 all-to-all-done.2
  63.1 9.3 %all-to-all-start.1 = ((bf16[32,2,9856]{2,1,0:T(2,128)(2,1)}), bf16[32,2,9856]{2,1,0:T(2,128)(2,1)S(1)}, u32[]{:S(2)}, u32[]{:S(2)}) async-start(bf16[32,2,9856]{2,1,0:T(2,128)(2,1)} %reshape.24), calls=%async_computation.1 | async-start | bytes 2523136 | tf_op jit(solution)/shard_map/all_to_all | solution.py:37
  72.4 1.0 dynamic-slice_bitcast_fusion
  73.4 1.3 copy.63
  74.7 3.2 %reshape.27 = bf16[256,8,44]{2,1,0:T(8,128)(2,1)} reshape(bf16[32,2,1408]{2,1,0:T(2,128)(2,1)} %all-to-all-done.2) | data formatting | bytes 360448
  77.9 2.0 %copy.55 = bf16[44,32,8,8]{0,3,2,1:T(8,128)(2,1)} copy(bf16[44,32,8,8]{0,2,3,1:T(8,128)(2,1)} %bitcast.47) | data formatting | bytes 360448 | tf_op jit(solution)/shard_map/all_to_all | solution.py:40
  79.8 2.2 %copy.56 = bf16[44,256,8]{1,2,0:T(8,128)(2,1)} copy(bf16[44,256,8]{0,2,1:T(8,128)(2,1)} %bitcast.48) | data formatting | bytes 360448 | tf_op jit(solution)/shard_map/all_to_all | solution.py:40
  82.0 19.5 %all-to-all-done.1 = bf16[32,2,9856]{2,1,0:T(2,128)(2,1)S(1)} async-done(((bf16[32,2,9856]{2,1,0:T(2,128)(2,1)}), bf16[32,2,9856]{2,1,0:T(2,128)(2,1)S(1)}, u32[]{:S(2)}, u32[]{:S(2)}) %all-to-all-start.1) | async-done | bytes 1261600 | tf_op jit(solution)/shard_map/all_to_all | solution.py:37
  101.5 5.6 %reshape.25 = bf16[256,44,56]{2,1,0:T(8,128)(2,1)} reshape(bf16[32,2,9856]{2,1,0:T(2,128)(2,1)S(1)} %all-to-all-done.1) | data formatting | bytes 2523136
  107.1 2.6 %convert_bitcast_fusion = f32[44,8,32,56]{3,1,2,0:T(8,128)S(1)} fusion(bf16[44,256,56]{2,0,1:T(8,128)(2,1)} %bitcast.40), kind=kLoop, calls=%fused_computation | loop fusion | flops 630784 | bytes 3784704 | tf_op jit(solution)/shard_map/convert_element_type | solution.py:39
  109.7 3.6 %copy.51 = f32[44,8,32,56]{3,2,1,0:T(8,128)} copy(f32[44,8,32,56]{3,1,2,0:T(8,128)S(1)} %convert_bitcast_fusion) | data formatting | bytes 5046272 | tf_op jit(solution)/shard_map/convert_element_type | solution.py:39
  113.4 6.3 %reshape.17 = f32[44,8,1792]{2,1,0:T(8,128)} reshape(f32[44,8,32,56]{3,2,1,0:T(8,128)} %copy.51) | data formatting | bytes 5046272 | tf_op jit(solution)/shard_map/convert_element_type | solution.py:39
  119.7 2.3 %fusion = bf16[44,8,1792]{2,1,0:T(8,128)(2,1)S(1)} fusion(f32[44,8,1792]{2,1,0:T(8,128)} %reshape.17, bf16[44,256,8]{1,2,0:T(8,128)(2,1)} %copy.56, bf16[256,1792,1]{0,1,2:T(8,128)(2,1)S(1)} %bitcast.45), kind=kOutput, calls=%fused_computation.2 | convolution fusion | flops 324222976 | bytes 4882432 | tf_op jit(solution)/shard_map/qji,ja->qia/dot_general | solution.py:41
  122.0 0.0 copy-start.1
  122.0 0.5 fusion.8
  122.5 15.3 %all_to_all.44 = f32[32,1,44]{2,1,0:T(1,128)S(1)} all-to-all(f32[32,1,44]{2,1,0:T(1,128)S(1)} %broadcast_in_dim.11), channel_id=1, replica_groups=mesh['pb'=8,'pq'=32] {'pq'}, dimensions={0} | all-to-all | bytes 11264 | tf_op jit(solution)/shard_map/all_to_all | solution.py:15
  137.8 0.3 multiply_reduce_fusion
  138.2 16.9 %all_to_all.45 = f32[8,8,1792]{2,1,0:T(8,128)S(1)} all-to-all(f32[8,8,1792]{2,1,0:T(8,128)S(1)} %broadcast_in_dim.12), channel_id=1, replica_groups=mesh['pb'=8,'pq'=32] {'pb'}, dimensions={0} | all-to-all | bytes 917504 | tf_op jit(solution)/shard_map/all_to_all | solution.py:15
  155.1 0.0 copy-done.1
  155.1 0.6 broadcast_multiply_fusion
  (4 shorter events, 0.1 us)
Async XLA Ops:
  0.6 36.4 %copy-start = (bf16[44,8,1792]{2,1,0:T(8,128)(2,1)S(1)}, bf16[44,8,1792]{2,1,0:T(8,128)(2,1)}, u32[]{:S(2)}) copy-start(bf16[44,8,1792]{2,1,0:T(8,128)(2,1)} %param.6) | copy-start | bytes 3784708
  0.6 36.4 %copy-start.2 = (bf16[44,8,256]{2,1,0:T(8,128)(2,1)S(1)}, bf16[44,8,256]{2,1,0:T(8,128)(2,1)}, u32[]{:S(2)}) copy-start(bf16[44,8,256]{2,1,0:T(8,128)(2,1)} %param.7) | copy-start | bytes 540676
  39.8 23.3 %all-to-all-start.2 = ((bf16[32,2,1408]{2,1,0:T(2,128)(2,1)}), bf16[32,2,1408]{2,1,0:T(2,128)(2,1)}, u32[]{:S(2)}, u32[]{:S(2)}) async-start(bf16[32,2,1408]{2,1,0:T(2,128)(2,1)} %reshape.26), calls=%async_computation.2 | async-start | bytes 360448 | tf_op jit(solution)/shard_map/all_to_all | solution.py:40
  63.1 38.4 %all-to-all-start.1 = ((bf16[32,2,9856]{2,1,0:T(2,128)(2,1)}), bf16[32,2,9856]{2,1,0:T(2,128)(2,1)S(1)}, u32[]{:S(2)}, u32[]{:S(2)}) async-start(bf16[32,2,9856]{2,1,0:T(2,128)(2,1)} %reshape.24), calls=%async_computation.1 | async-start | bytes 2523136 | tf_op jit(solution)/shard_map/all_to_all | solution.py:37
  122.0 33.1 %copy-start.1 = (bf16[44,8,1792]{2,1,0:T(8,128)(2,1)}, bf16[44,8,1792]{2,1,0:T(8,128)(2,1)S(1)}, u32[]{:S(2)}) copy-start(bf16[44,8,1792]{2,1,0:T(8,128)(2,1)S(1)} %fusion) | copy-start | bytes 3784708
where the time goes:
time: 157 us; the launch traced here: 156 us
  blocking collectives  67.6 us (43%)
  local copies, waits for them, and re-layouts  39.2 us (25%)
  waiting for transfers between devices  19.5 us (12%)
  starting transfers between devices  15.4 us (10%)
  matrix products  9.58 us (6%)
  other arithmetic  3.61 us (2%)
    all_to_all x3, blocking collectives, copy_for_each(): return lax.all_to_all(copies, axis, split_axis=0, concat_axis=0, tiled=True)  67.6 us
    all_to_all x1, waiting for transfers between devices, per_device(): lax.all_to_all(partial_sum.astype(jnp.bfloat16), 'pq', split_axis=1, conc...  19.5 us
    unnamed x10, local copies, waits for them, and re-layouts  17.1 us
    convert_element_type x2, local copies, waits for them, and re-layouts, per_device(): moved_sum = lax.all_to_all(partial_sum.astype(jnp.bfloat16), 'pq', split_...  9.91 us
    all_to_all x1, starting transfers between devices, per_device(): lax.all_to_all(partial_sum.astype(jnp.bfloat16), 'pq', split_axis=1, conc...  9.33 us
    dot_general x1, matrix products, per_device(): jnp.einsum('qab,ib->qia', chol_vv, whole_amps, preferred_element_type=jnp...  6.27 us
    all_to_all x1, starting transfers between devices, per_device(): lax.all_to_all(lprime, 'pq', split_axis=2, concat_axis=1, tiled=True)  6.1 us
    convert_element_type x1, local copies, waits for them, and re-layouts, per_device(): partial_sum.astype(jnp.bfloat16)  4.5 us
  transfers between devices with their start and end apart: 2, of which 1 were waited for; matrix products, arithmetic and copies ran while one was open for 17% of the time, Pallas kernels for 0%

commit v1 on v0

v1 whole, which is shorter than its diff:
```python
import jax
import jax.numpy as jnp
from jax import lax
from jax.experimental import pallas as pl
from jax.experimental.pallas import tpu as pltpu
from jax.sharding import PartitionSpec as P

NZ, NY = 8, 4
LANES = 128
OWN_I = 8
GROUP = LANES // OWN_I
F32, BF16 = jnp.float32, jnp.bfloat16
NT = (((1,), (1,)), ((), ()))
TN = (((0,), (0,)), ((), ()))


def z_groups():
    return [[z * NY + y for z in range(NZ)] for y in range(NY)]


def y_shift(k):
    return [(z * NY + y, z * NY + (y + k) % NY) for z in range(NZ) for y in range(NY)]


def split3(x):
    hi = x.astype(BF16)
    rest = x - hi.astype(F32)
    mid = rest.astype(BF16)
    low = (rest - mid.astype(F32)).astype(BF16)
    return hi, mid, low


def swap_blocks(tiles):
    lane = lax.broadcasted_iota(jnp.int32, tiles[0].shape, 1)
    bit = 1
    while bit < GROUP:
        upper = (lane // OWN_I) & bit != 0
        out = list(tiles)
        for q in range(GROUP):
            if q & bit:
                continue
            low, high = tiles[q], tiles[q | bit]
            out[q] = jnp.where(upper, pltpu.roll(high, OWN_I * bit, 1), low)
            out[q | bit] = jnp.where(upper, high, pltpu.roll(low, LANES - OWN_I * bit, 1))
        tiles = out
        bit *= 2
    return tiles


def send_side(vv, ov, oo, vo, own, p0, p1, p2, p3, out, tt, d, gram):
    nq, n_own, nocc = vo.shape
    rows = n_own + OWN_I
    full = nq // GROUP * GROUP
    me = lax.axis_index("pq")
    y = me % NY
    for k, piece in enumerate((p0, p1, p2, p3)):
        src = (y - k + NY) % NY
        for z in range(NZ):
            tt[pl.ds(pl.multiple_of((z * NY + src) * n_own, 8), n_own), :] = piece[z]
    amps = tt[...]
    gram[...] = lax.dot_general(amps, amps, TN, preferred_element_type=F32)
    weight = jnp.concatenate(
        [own[...].astype(F32), -gram[pl.ds(pl.multiple_of(me * OWN_I, 8), OWN_I), :]], 0
    )
    lp = jnp.dot(ov[...], amps, preferred_element_type=F32).reshape(nq, OWN_I, nocc)
    d[:, n_own:, :] = (lp + oo[...].astype(F32)).astype(BF16).astype(F32)
    share = []
    for q0 in range(0, nq, GROUP):
        q1 = min(nq, q0 + GROUP)
        part = jnp.dot(vv[q0 * n_own : q1 * n_own, :], amps, preferred_element_type=F32)
        d[q0:q1, :n_own, :] = part.reshape(q1 - q0, n_own, nocc) + vo[q0:q1].astype(F32)
    half = GROUP // 2
    for t in range(nq // GROUP):
        for h in range(nocc // LANES):
            for r in range(0, rows, 16):
                tiles = [
                    d[t * GROUP + q, r : r + 16, h * LANES : (h + 1) * LANES]
                    for q in range(GROUP)
                ]
                for g, tile in enumerate(swap_blocks(tiles)):
                    out[h * GROUP + g, t * rows + r : t * rows + r + 16, :] = tile.astype(BF16)
    left = nq - full
    spare = GROUP - left
    short = rows - 16
    for h in range(nocc // LANES):
        cols = slice(h * LANES, (h + 1) * LANES)
        for n, r in enumerate(range(0, short, 16)):
            tiles = [d[full + q, r : r + 16, cols] for q in range(left)]
            tiles += [d[full + n * spare + v, short:rows, cols] for v in range(spare)]
            for g, tile in enumerate(swap_blocks(tiles)):
                at = full // GROUP * rows + r
                out[h * GROUP + g, at : at + 16, :] = tile.astype(BF16)
    lane = lax.broadcasted_iota(jnp.int32, (1, LANES), 1)
    row = jnp.zeros((1, LANES), F32)
    for q in range(nq):
        total = jnp.sum(d[q] * weight, axis=(0, 1), keepdims=True)
        row = jnp.where(lane == q, 2.0 * total, row)
    block = jnp.concatenate(
        [s.astype(F32) for s in split3(row)] + [jnp.zeros((8 - 3, LANES), F32)], 0
    ).astype(BF16)
    at = full // GROUP * rows + short
    for p in range(out.shape[0]):
        out[p, at : at + 8, :] = block


def receive_side(got, tt, dressed, fock, raw, lpt):
    n_dev = got.shape[0]
    nq = dressed.shape[0] // OWN_I
    nvirt = tt.shape[0]
    n_own = nvirt // n_dev
    rows = n_own + OWN_I
    full = nq // GROUP * GROUP
    n_full = full // GROUP
    left = nq - full
    spare = GROUP - left
    short = rows - 16
    lane16 = lax.broadcasted_iota(jnp.int32, (16, LANES), 1)
    width = spare * OWN_I
    for p in range(n_dev):
        a = p * n_own
        for t in range(n_full):
            raw[a : a + n_own, t * LANES : (t + 1) * LANES] = got[p, t * rows : t * rows + n_own, :]
            lpt[p * OWN_I : (p + 1) * OWN_I, t * LANES : (t + 1) * LANES] = got[
                p, t * rows + n_own : (t + 1) * rows, :
            ]
        base = n_full * rows
        tail = jnp.zeros((16, LANES), F32)
        for n in range(short // 16):
            part = pltpu.roll(
                got[p, base + 16 * n : base + 16 * (n + 1), :].astype(F32), (n + 1) * width, 1
            )
            here = (lane16 >= n * width) & (lane16 < (n + 1) * width)
            tail = jnp.where(here, part, tail)
        raw[a : a + short, n_full * LANES :] = got[p, base : base + short, :]
        raw[a + short : a + n_own, n_full * LANES :] = tail[: n_own - short].astype(BF16)
        lpt[p * OWN_I : (p + 1) * OWN_I, n_full * LANES :] = tail[n_own - short :].astype(BF16)
    lanes_in = (n_full + 1) * LANES
    m = nq * OWN_I
    eye = (
        lax.broadcasted_iota(jnp.int32, (m, lanes_in), 0)
        == lax.broadcasted_iota(jnp.int32, (m, lanes_in), 1)
    ).astype(F32).astype(BF16)
    lp = lax.dot_general(eye, lpt[...], NT, preferred_element_type=F32).astype(BF16)
    moved = lax.dot_general(eye, raw[...], NT, preferred_element_type=F32)
    occupied = lax.dot_general(lp, tt[...], NT, preferred_element_type=F32)
    result = (moved - occupied).astype(BF16)
    dressed[...] = result
    at = n_full * rows + short
    shares = jnp.sum(got[:, at : at + 8, :].astype(F32), axis=0)
    coulomb = shares[0:1] + shares[1:2] + shares[2:3]
    pick = lax.broadcasted_iota(jnp.int32, (m, LANES), 1) == lax.broadcasted_iota(
        jnp.int32, (m, LANES), 0
    ) // OWN_I
    column = jnp.sum(jnp.where(pick, coulomb, 0.0), axis=1, keepdims=True)
    fock[...] = jnp.sum((column * result.astype(F32)).reshape(nq, OWN_I, nvirt), axis=0).astype(
        fock.dtype
    )


VMEM = pl.BlockSpec(memory_space=pltpu.VMEM)
PARAMS = pltpu.CompilerParams(vmem_limit_bytes=56 * 1024 * 1024)


def per_device(chol_vv, chol_ov, chol_oo, chol_vo, amplitudes):
    nq, n_own, nvirt = chol_vv.shape
    nocc = amplitudes.shape[0]
    n_dev = lax.axis_size("pq")
    own = amplitudes.T
    near = lax.all_to_all(
        jnp.broadcast_to(own, (NZ, n_own, nocc)), "pq", 0, 0, axis_index_groups=z_groups(), tiled=True
    )
    pieces = [near] + [lax.ppermute(near, "pq", y_shift(k)) for k in range(1, NY)]
    rows = n_own + OWN_I
    sent_rows = nq * rows * OWN_I // LANES + 8
    sent, tt = pl.pallas_call(
        send_side,
        out_shape=(
            jax.ShapeDtypeStruct((n_dev, sent_rows, LANES), BF16),
            jax.ShapeDtypeStruct((nvirt, nocc), BF16),
        ),
        in_specs=[VMEM] * 9,
        out_specs=(VMEM, VMEM),
        scratch_shapes=[pltpu.VMEM((nq, rows, nocc), F32), pltpu.VMEM((nocc, nocc), F32)],
        compiler_params=PARAMS,
        name="send_side",
    )(
        chol_vv.reshape(nq * n_own, nvirt),
        chol_ov.reshape(nq * OWN_I, nvirt),
        chol_oo,
        chol_vo.transpose(0, 2, 1),
        own,
        *pieces,
    )
    got = lax.all_to_all(sent, "pq", 0, 0, tiled=True)
    lanes_in = -(-nq // GROUP) * LANES
    dressed, fock = pl.pallas_call(
        receive_side,
        out_shape=(
            jax.ShapeDtypeStruct((nq * OWN_I, nvirt), BF16),
            jax.ShapeDtypeStruct((OWN_I, nvirt), BF16),
        ),
        in_specs=[VMEM] * 2,
        out_specs=(VMEM, VMEM),
        scratch_shapes=[pltpu.VMEM((nvirt, lanes_in), BF16), pltpu.VMEM((nocc, lanes_in), BF16)],
        compiler_params=PARAMS,
        name="receive_side",
    )(got, tt)
    n_pb = lax.axis_size("pb")
    parts = lax.all_to_all(jnp.broadcast_to(fock, (n_pb, *fock.shape)), "pb", 0, 0, tiled=True)
    fock_ov = jnp.sum(parts.astype(F32), axis=0) / (nq * n_pb)
    return dressed.reshape(nq, OWN_I, nvirt), fock_ov


def solution(mesh):
    in_specs = (
        P("pb", "pq", None),
        P("pb", "pq", None),
        P("pb", "pq", None),
        P("pb", None, "pq"),
        P(None, "pq"),
    )
    out_specs = (P("pb", "pq", None), P("pq", None))
    return jax.shard_map(
        per_device, mesh=mesh, in_specs=in_specs, out_specs=out_specs, check_vma=False
    )
```

time: 157 us -> 108 us (0.69)
  local copies, waits for them, and re-layouts: 39.2 us -> 2.22 us
  Pallas kernels: 0 us -> 14.3 us
  starting transfers between devices: 15.4 us -> 3.77 us
  matrix products: 9.58 us -> 0 us
  waiting for transfers between devices: 19.5 us -> 12.2 us
  blocking collectives: 67.6 us -> 73.4 us
  other arithmetic: 3.61 us -> 0.66 us
    all_to_all x2 -> x0, waiting for transfers between devices: 19.5 us -> none  [the longest x1 19.5 us: per_device(): lax.all_to_all(partial_sum.astype(jnp.bfloat16), 'pq', split_axis=1, conc...]
    unnamed x10 -> x8, local copies, waits for them, and re-layouts: 17.1 us -> 0.7 us
    all_to_all x2 -> x0, starting transfers between devices: 15.4 us -> none  [the longest x1 9.33 us: per_device(): lax.all_to_all(partial_sum.astype(jnp.bfloat16), 'pq', split_axis=1, conc...]
    convert_element_type x4 -> x0, local copies, waits for them, and re-layouts: 14.8 us -> none  [the longest x2 9.91 us: per_device(): moved_sum = lax.all_to_all(partial_sum.astype(jnp.bfloat16), 'pq', split_...]
    pallas_call x0 -> x2, Pallas kernels: none -> 14.3 us  [the longest x1 10.2 us: per_device(): pl.pallas_call(send_side, out_shape=(jax.ShapeDtypeStruct((n_dev, sent_ro...]
    ppermute x0 -> x3, waiting for transfers between devices: none -> 12.2 us  [per_device(): lax.ppermute(near, 'pq', y_shift(k))]
    dot_general x4 -> x0, matrix products: 9.58 us -> none  [the longest x1 6.27 us: per_device(): jnp.einsum('qab,ib->qia', chol_vv, whole_amps, preferred_element_type=jnp...]
    all_to_all x3, blocking collectives: 67.6 us -> 73.4 us  [the longest x1 41.4 us: per_device(): got = lax.all_to_all(sent, 'pq', 0, 0, tiled=True)]
  transfers between devices with their start and end apart: 2 -> 3, of which waited for: 1 -> 3; matrix products, arithmetic and copies ran while one was open for 17% -> 0% of each run, Pallas kernels for 0% -> 0%
where the time goes in v1:
time: 108 us; the launch traced here: 107 us
  blocking collectives  73.4 us (68%)
  Pallas kernels  14.3 us (13%)
  waiting for transfers between devices  12.2 us (11%)
  starting transfers between devices  3.77 us (3%)
  local copies, waits for them, and re-layouts  2.22 us (2%)
    all_to_all x1, blocking collectives, per_device(): got = lax.all_to_all(sent, 'pq', 0, 0, tiled=True)  41.4 us
    all_to_all x1, blocking collectives, per_device(): lax.all_to_all(jnp.broadcast_to(own, (NZ, n_own, nocc)), 'pq', 0, 0, axis...  18.6 us
    all_to_all x1, blocking collectives, per_device(): lax.all_to_all(jnp.broadcast_to(fock, (n_pb, *fock.shape)), 'pb', 0, 0, t...  13.4 us
    ppermute x3, waiting for transfers between devices, per_device(): lax.ppermute(near, 'pq', y_shift(k))  12.2 us
    pallas_call x1, Pallas kernels, per_device(): pl.pallas_call(send_side, out_shape=(jax.ShapeDtypeStruct((n_dev, sent_ro...  10.2 us
    pallas_call x1, Pallas kernels, per_device(): pl.pallas_call(receive_side, out_shape=(jax.ShapeDtypeStruct((nq * OWN_I,...  4.08 us
    ppermute x3, starting transfers between devices, per_device(): lax.ppermute(near, 'pq', y_shift(k))  3.77 us
  transfers between devices with their start and end apart: 3, of which 3 were waited for; matrix products, arithmetic and copies ran while one was open for 0% of the time, Pallas kernels for 0%

profile of v1, /device:TPU:1, one launch (start us, length us, event | category | flops | bytes accessed | tf_op | source)
XLA Modules:
  0.0 107.3 jit_solution(12098177577561470370)
XLA Ops:
  0.6 0.8 broadcast_in_dim.6
  1.4 18.6 %all_to_all.15.p0 = bf16[8,56,256]{2,1,0:T(8,128)(2,1)S(1)} all-to-all(bf16[8,56,256]{2,1,0:T(8,128)(2,1)S(1)} %broadcast_in_dim.6), channel_id=1, replica_groups={{0,4,8,12,16,20,24,28},{1,5,9,13,17,21,25,29},{2,6,10,14,18,22,26,30},{..., dimensions={0} | all-to-all | bytes 458752 | tf_op jit(solution)/shard_map/all_to_all | solution.py:169
  20.0 0.0 copy-start
  20.0 2.7 %collective-permute-start.2 = (bf16[8,56,256]{2,1,0:T(8,128)(2,1)S(1)}, bf16[8,56,256]{2,1,0:T(8,128)(2,1)S(1)}, u32[]{:S(2)}, u32[]{:S(2)}) collective-permute-start(bf16[8,56,256]{2,1,0:T(8,128)(2,1)S(1)} %all_to_all.15.p0), channel_id=1, source_target_pairs={{0,3},{1,0},{2,1},{3,2},{4,7},{5,4},{6,5},{7,6},{8,11},{9,8},{10,9... | collective-permute-start | bytes 688136 | tf_op jit(solution)/shard_map/ppermute | solution.py:172
  22.8 0.3 collective-permute-start.1
  23.1 0.7 collective-permute-start
  23.8 4.8 %collective-permute-done.2.p3 = bf16[8,56,256]{2,1,0:T(8,128)(2,1)S(1)} collective-permute-done((bf16[8,56,256]{2,1,0:T(8,128)(2,1)S(1)}, bf16[8,56,256]{2,1,0:T(8,128)(2,1)S(1)}, u32[]{:S(2)}, u32[]{:S(2)}) %collective-permute-start.2) | collective-permute-done | bytes 229408 | tf_op jit(solution)/shard_map/ppermute | solution.py:172
  28.6 0.0 copy-start.1
  28.6 0.6 collective-permute-done.1.p2
  29.2 0.0 copy-start.2
  29.2 6.8 %collective-permute-done.p1 = bf16[8,56,256]{2,1,0:T(8,128)(2,1)S(1)} collective-permute-done((bf16[8,56,256]{2,1,0:T(8,128)(2,1)S(1)}, bf16[8,56,256]{2,1,0:T(8,128)(2,1)S(1)}, u32[]{:S(2)}, u32[]{:S(2)}) %collective-permute-start) | collective-permute-done | bytes 229408 | tf_op jit(solution)/shard_map/ppermute | solution.py:172
  36.0 0.0 copy-start.3
  36.0 0.0 copy-done
  36.0 0.0 copy-done.1
  36.0 0.0 copy-done.2
  36.0 0.7 copy-done.3
  36.7 10.2 %send_side.1 = (bf16[32,184,128]{2,1,0:T(8,128)(2,1)}, bf16[1792,256]{1,0:T(8,128)(2,1)}) custom-call(bf16[2464,1792]{1,0:T(8,128)(2,1)} %bitcast.5, bf16[352,1792]{1,0:T(8,128)(2,1)} %bitcast.6, bf16[44,8,256]{2,1,0:T(8,128)(2,1)} %oo.1, bf16[44,56,256]{2,1,0:T(8,128)(2,1)} %bitcast.7, bf16[56,256]{1,0:T(8,128)(2,1)} %bitcast.9, ...), custom_call_target="tpu_custom_call" | custom-call | tf_op jit(solution)/shard_map/send_side/pallas_call | solution.py:175
  46.9 41.4 %all_to_all.16.got = bf16[32,184,128]{2,1,0:T(8,128)(2,1)} all-to-all(bf16[32,184,128]{2,1,0:T(8,128)(2,1)} %get-tuple-element.6), channel_id=1, replica_groups=mesh['pb'=8,'pq'=32] {'pq'}, dimensions={0} | all-to-all | bytes 3014656 | tf_op jit(solution)/shard_map/all_to_all | solution.py:194
  88.4 4.1 %receive_side.1 = (bf16[352,1792]{1,0:T(8,128)(2,1)}, bf16[8,1792]{1,0:T(8,128)(2,1)}) custom-call(bf16[32,184,128]{2,1,0:T(8,128)(2,1)} %all_to_all.16.got, bf16[1792,256]{1,0:T(8,128)(2,1)} %get-tuple-element.7.tt), custom_call_target="tpu_custom_call" | custom-call | tf_op jit(solution)/shard_map/receive_side/pallas_call | solution.py:196
  92.5 0.8 broadcast_in_dim.7
  93.2 13.4 %all_to_all.17 = bf16[8,8,1792]{2,1,0:T(8,128)(2,1)S(1)} all-to-all(bf16[8,8,1792]{2,1,0:T(8,128)(2,1)S(1)} %broadcast_in_dim.7), channel_id=1, replica_groups=mesh['pb'=8,'pq'=32] {'pb'}, dimensions={0} | all-to-all | bytes 458752 | tf_op jit(solution)/shard_map/all_to_all | solution.py:209
  106.7 0.6 broadcast_multiply_fusion
  (1 shorter events, 0.0 us)
Async XLA Ops:
  20.0 16.0 %copy-start = (bf16[8,56,256]{2,1,0:T(8,128)(2,1)}, bf16[8,56,256]{2,1,0:T(8,128)(2,1)S(1)}, u32[]{:S(2)}) copy-start(bf16[8,56,256]{2,1,0:T(8,128)(2,1)S(1)} %all_to_all.15.p0) | copy-start | bytes 688132
  20.0 8.6 %collective-permute-start.2 = (bf16[8,56,256]{2,1,0:T(8,128)(2,1)S(1)}, bf16[8,56,256]{2,1,0:T(8,128)(2,1)S(1)}, u32[]{:S(2)}, u32[]{:S(2)}) collective-permute-start(bf16[8,56,256]{2,1,0:T(8,128)(2,1)S(1)} %all_to_all.15.p0), channel_id=1, source_target_pairs={{0,3},{1,0},{2,1},{3,2},{4,7},{5,4},{6,5},{7,6},{8,11},{9,8},{10,9... | collective-permute-start | bytes 688136 | tf_op jit(solution)/shard_map/ppermute | solution.py:172
  22.8 6.5 %collective-permute-start.1 = (bf16[8,56,256]{2,1,0:T(8,128)(2,1)S(1)}, bf16[8,56,256]{2,1,0:T(8,128)(2,1)S(1)}, u32[]{:S(2)}, u32[]{:S(2)}) collective-permute-start(bf16[8,56,256]{2,1,0:T(8,128)(2,1)S(1)} %all_to_all.15.p0), channel_id=1, source_target_pairs={{0,2},{1,3},{2,0},{3,1},{4,6},{5,7},{6,4},{7,5},{8,10},{9,11},{10,... | collective-permute-start | bytes 688136 | tf_op jit(solution)/shard_map/ppermute | solution.py:172
  23.1 12.9 %collective-permute-start = (bf16[8,56,256]{2,1,0:T(8,128)(2,1)S(1)}, bf16[8,56,256]{2,1,0:T(8,128)(2,1)S(1)}, u32[]{:S(2)}, u32[]{:S(2)}) collective-permute-start(bf16[8,56,256]{2,1,0:T(8,128)(2,1)S(1)} %all_to_all.15.p0), channel_id=1, source_target_pairs={{0,1},{1,2},{2,3},{3,0},{4,5},{5,6},{6,7},{7,4},{8,9},{9,10},{10,1... | collective-permute-start | bytes 688136 | tf_op jit(solution)/shard_map/ppermute | solution.py:172
  28.6 7.4 %copy-start.1 = (bf16[8,56,256]{2,1,0:T(8,128)(2,1)}, bf16[8,56,256]{2,1,0:T(8,128)(2,1)S(1)}, u32[]{:S(2)}) copy-start(bf16[8,56,256]{2,1,0:T(8,128)(2,1)S(1)} %collective-permute-done.2.p3) | copy-start | bytes 688132
  29.2 6.8 %copy-start.2 = (bf16[8,56,256]{2,1,0:T(8,128)(2,1)}, bf16[8,56,256]{2,1,0:T(8,128)(2,1)S(1)}, u32[]{:S(2)}) copy-start(bf16[8,56,256]{2,1,0:T(8,128)(2,1)S(1)} %collective-permute-done.1.p2) | copy-start | bytes 688132
  36.0 0.7 copy-start.3

commit v2 on v1

--- a/solution.py
+++ b/solution.py
@@ -1,3 +1,5 @@
+import functools
+
 import jax
 import jax.numpy as jnp
 from jax import lax
@@ -47,51 +49,69 @@
     return tiles
 
 
-def send_side(vv, ov, oo, vo, own, p0, p1, p2, p3, out, tt, d, gram):
+def touch(near, vv, ov, oo, vo, token):
+    del near, vv, ov, oo, vo
+    token[...] = jnp.zeros_like(token)
+
+
+def send_side(token, vv, ov, oo, vo, own, *refs):
+    del token
+    pieces, (out, tt, d, gram) = refs[: 2 * NY], refs[2 * NY :]
     nq, n_own, nocc = vo.shape
     rows = n_own + OWN_I
     full = nq // GROUP * GROUP
     me = lax.axis_index("pq")
-    y = me % NY
-    for k, piece in enumerate((p0, p1, p2, p3)):
-        src = (y - k + NY) % NY
-        for z in range(NZ):
-            tt[pl.ds(pl.multiple_of((z * NY + src) * n_own, 8), n_own), :] = piece[z]
+    core = lax.axis_index("pb") & 1
+    y = me & (NY - 1)
+    half = pieces[0].shape[1]
+    for k in range(NY):
+        src = (y - k + NY) & (NY - 1)
+        for c in range(2):
+            shift = (core if c == 0 else 1 - core) * (n_own - half)
+            for z in range(NZ):
+                at = pl.multiple_of((z * NY + src) * n_own + shift, 8)
+                tt[pl.ds(at, half), :] = pieces[2 * k + c][z]
     amps = tt[...]
-    gram[...] = lax.dot_general(amps, amps, TN, preferred_element_type=F32)
-    weight = jnp.concatenate(
-        [own[...].astype(F32), -gram[pl.ds(pl.multiple_of(me * OWN_I, 8), OWN_I), :]], 0
-    )
     lp = jnp.dot(ov[...], amps, preferred_element_type=F32).reshape(nq, OWN_I, nocc)
     d[:, n_own:, :] = (lp + oo[...].astype(F32)).astype(BF16).astype(F32)
-    share = []
-    for q0 in range(0, nq, GROUP):
-        q1 = min(nq, q0 + GROUP)
+
+    def dress(t):
+        q0, q1 = t * GROUP, min(nq, (t + 1) * GROUP)
         part = jnp.dot(vv[q0 * n_own : q1 * n_own, :], amps, preferred_element_type=F32)
         d[q0:q1, :n_own, :] = part.reshape(q1 - q0, n_own, nocc) + vo[q0:q1].astype(F32)
-    half = GROUP // 2
-    for t in range(nq // GROUP):
-        for h in range(nocc // LANES):
-            for r in range(0, rows, 16):
-                tiles = [
-                    d[t * GROUP + q, r : r + 16, h * LANES : (h + 1) * LANES]
-                    for q in range(GROUP)
-                ]
-                for g, tile in enumerate(swap_blocks(tiles)):
-                    out[h * GROUP + g, t * rows + r : t * rows + r + 16, :] = tile.astype(BF16)
+
     left = nq - full
     spare = GROUP - left
     short = rows - 16
-    for h in range(nocc // LANES):
-        cols = slice(h * LANES, (h + 1) * LANES)
-        for n, r in enumerate(range(0, short, 16)):
-            tiles = [d[full + q, r : r + 16, cols] for q in range(left)]
-            tiles += [d[full + n * spare + v, short:rows, cols] for v in range(spare)]
-            for g, tile in enumerate(swap_blocks(tiles)):
-                at = full // GROUP * rows + r
-                out[h * GROUP + g, at : at + 16, :] = tile.astype(BF16)
+
+    def pack(t):
+        for h in range(nocc // LANES):
+            cols = slice(h * LANES, (h + 1) * LANES)
+            for r in range(0, rows if t * GROUP < full else short, 8):
+                if t * GROUP < full:
+                    tiles = [d[t * GROUP + q, r : r + 8, cols] for q in range(GROUP)]
+                else:
+                    n, r2 = divmod(r, 16)
+                    tiles = [d[full + q, r : r + 8, cols] for q in range(left)]
+                    tiles += [
+                        d[full + n * spare + v, short + r2 : short + r2 + 8, cols]
+                        for v in range(spare)
+                    ]
+                for g, tile in enumerate(swap_blocks(tiles)):
+                    out[h * GROUP + g, t * rows + r : t * rows + r + 8, :] = tile.astype(BF16)
+
     lane = lax.broadcasted_iota(jnp.int32, (1, LANES), 1)
     row = jnp.zeros((1, LANES), F32)
+    n_tiles = -(-nq // GROUP)
+    dress(0)
+    for t in range(1, n_tiles):
+        dress(t)
+        pack(t - 1)
+    gram[...] = lax.dot_general(amps, amps, TN, preferred_element_type=F32)
+    pack(n_tiles - 1)
+    weight = jnp.concatenate(
+        [own[...].astype(F32), -gram[pl.ds(pl.multiple_of(me * OWN_I, 8), OWN_I), :]], 0
+    )
     for q in range(nq):
         total = jnp.sum(d[q] * weight, axis=(0, 1), keepdims=True)
         row = jnp.where(lane == q, 2.0 * total, row)
@@ -103,7 +123,7 @@
         out[p, at : at + 8, :] = block
 
 
-def receive_side(got, tt, dressed, fock, raw, lpt):
+def receive_side(scale, got, tt, dressed, fock, raw, lpt):
     n_dev = got.shape[0]
     nq = dressed.shape[0] // OWN_I
     nvirt = tt.shape[0]
@@ -152,24 +172,47 @@
         jnp.int32, (m, LANES), 0
     ) // OWN_I
     column = jnp.sum(jnp.where(pick, coulomb, 0.0), axis=1, keepdims=True)
-    fock[...] = jnp.sum((column * result.astype(F32)).reshape(nq, OWN_I, nvirt), axis=0).astype(
-        fock.dtype
-    )
+    part = jnp.sum((column * result.astype(F32)).reshape(nq, OWN_I, nvirt), axis=0) * scale
+    for copy in range(fock.shape[0]):
+        fock[copy] = part.astype(fock.dtype)
 
 
 VMEM = pl.BlockSpec(memory_space=pltpu.VMEM)
-PARAMS = pltpu.CompilerParams(vmem_limit_bytes=56 * 1024 * 1024)
+ANY = pl.BlockSpec(memory_space=pl.ANY)
+PARAMS = pltpu.CompilerParams(vmem_limit_bytes=26 * 1024 * 1024)
 
 
 def per_device(chol_vv, chol_ov, chol_oo, chol_vo, amplitudes):
     nq, n_own, nvirt = chol_vv.shape
     nocc = amplitudes.shape[0]
-    n_dev = lax.axis_size("pq")
+    n_dev, n_pb = lax.axis_size("pq"), lax.axis_size("pb")
     own = amplitudes.T
+    half = -(-n_own // 16) * 8
+    core = lax.axis_index("pb") & 1
+    mine = jnp.where(core == 0, own[:half], own[n_own - half :])
     near = lax.all_to_all(
-        jnp.broadcast_to(own, (NZ, n_own, nocc)), "pq", 0, 0, axis_index_groups=z_groups(), tiled=True
-    )
-    pieces = [near] + [lax.ppermute(near, "pq", y_shift(k)) for k in range(1, NY)]
+        jnp.broadcast_to(mine, (NZ, half, nocc)), "pq", 0, 0, axis_index_groups=z_groups(), tiled=True
+    )
+    other = [(b, b ^ 1) for b in range(n_pb)]
+    pieces = [near]
+    for k in range(1, NY):
+        pieces.append(lax.ppermute(near, "pq", y_shift(k)))
+    pieces = [p for piece in pieces for p in (piece, lax.ppermute(piece, "pb", other))]
+    blocks = (
+        chol_vv.reshape(nq * n_own, nvirt),
+        chol_ov.reshape(nq * OWN_I, nvirt),
+        chol_oo,
+        chol_vo.transpose(0, 2, 1),
+    )
+    token = pl.pallas_call(
+        touch,
+        out_shape=jax.ShapeDtypeStruct((8, LANES), F32),
+        in_specs=[ANY] * 5,
+        out_specs=VMEM,
+        compiler_params=PARAMS,
+        cost_estimate=pl.CostEstimate(flops=4_000_000_000, bytes_accessed=0, transcendentals=0),
+        name="touch",
+    )(near, *blocks)
     rows = n_own + OWN_I
     sent_rows = nq * rows * OWN_I // LANES + 8
     sent, tt = pl.pallas_call(
@@ -178,26 +221,19 @@
             jax.ShapeDtypeStruct((n_dev, sent_rows, LANES), BF16),
             jax.ShapeDtypeStruct((nvirt, nocc), BF16),
         ),
-        in_specs=[VMEM] * 9,
+        in_specs=[ANY] + [VMEM] * (5 + 2 * NY),
         out_specs=(VMEM, VMEM),
         scratch_shapes=[pltpu.VMEM((nq, rows, nocc), F32), pltpu.VMEM((nocc, nocc), F32)],
         compiler_params=PARAMS,
         name="send_side",
-    )(
-        chol_vv.reshape(nq * n_own, nvirt),
-        chol_ov.reshape(nq * OWN_I, nvirt),
-        chol_oo,
-        chol_vo.transpose(0, 2, 1),
-        own,
-        *pieces,
-    )
+    )(token, *blocks, own, *pieces)
     got = lax.all_to_all(sent, "pq", 0, 0, tiled=True)
     lanes_in = -(-nq // GROUP) * LANES
     dressed, fock = pl.pallas_call(
-        receive_side,
+        functools.partial(receive_side, 1.0 / (nq * n_pb)),
         out_shape=(
             jax.ShapeDtypeStruct((nq * OWN_I, nvirt), BF16),
-            jax.ShapeDtypeStruct((OWN_I, nvirt), BF16),
+            jax.ShapeDtypeStruct((n_pb, OWN_I, nvirt), BF16),
         ),
         in_specs=[VMEM] * 2,
         out_specs=(VMEM, VMEM),
@@ -205,9 +241,8 @@
         compiler_params=PARAMS,
         name="receive_side",
     )(got, tt)
-    n_pb = lax.axis_size("pb")
-    parts = lax.all_to_all(jnp.broadcast_to(fock, (n_pb, *fock.shape)), "pb", 0, 0, tiled=True)
-    fock_ov = jnp.sum(parts.astype(F32), axis=0) / (nq * n_pb)
+    parts = lax.all_to_all(fock, "pb", 0, 0, tiled=True)
+    fock_ov = jnp.sum(parts.astype(F32), axis=0)
     return dressed.reshape(nq, OWN_I, nvirt), fock_ov
 
 
@@ -220,6 +255,5 @@
         P(None, "pq"),
     )
     out_specs = (P("pb", "pq", None), P("pq", None))
-    return jax.shard_map(
-        per_device, mesh=mesh, in_specs=in_specs, out_specs=out_specs, check_vma=False
-    )
+
+    return jax.shard_map(per_device, mesh=mesh, in_specs=in_specs, out_specs=out_specs, check_vma=False)

time: 108 us -> 98.7 us (0.914)
  waiting for transfers between devices: 12.2 us -> 0.02 us
  starting transfers between devices: 3.77 us -> 13.2 us
  Pallas kernels: 14.3 us -> 6.23 us
  local copies, waits for them, and re-layouts: 2.22 us -> 7.75 us
  blocking collectives: 73.4 us -> 68.9 us
    ppermute x3 -> x7, waiting for transfers between devices: 12.2 us -> 0.02 us  [the longest x4 0.01 us: per_device(): lax.ppermute(piece, 'pb', other)]
    ppermute x3 -> x7, starting transfers between devices: 3.77 us -> 13.2 us  [the longest x4 9.4 us: per_device(): lax.ppermute(piece, 'pb', other)]
    unnamed x8 -> x10, local copies, waits for them, and re-layouts: 0.7 us -> 7.74 us
    pallas_call x1, Pallas kernels: 10.2 us -> 3.77 us  [per_device(): pl.pallas_call(send_side, out_shape=(jax.ShapeDtypeStruct((n_dev, sent_ro...]
    all_to_all x2, blocking collectives: 32 us -> 27.3 us  [the longest x1 16.6 us: per_device(): lax.all_to_all(jnp.broadcast_to(mine, (NZ, half, nocc)), 'pq', 0, 0, axis...]
    pallas_call x1 -> x2, Pallas kernels: 4.08 us -> 2.47 us  [the longest x1 2.47 us: per_device(): pl.pallas_call(functools.partial(receive_side, 1.0 / (nq * n_pb)), out_sh...]
    broadcast_in_dim x2 -> x1, local copies, waits for them, and re-layouts: 1.53 us -> 0.01 us  [per_device(): jnp.broadcast_to(mine, (NZ, half, nocc))]
  transfers between devices with their start and end apart: 3 -> 7, of which waited for: 3 -> 0; matrix products, arithmetic and copies ran while one was open for 0% -> 0% of each run, Pallas kernels for 0% -> 0%
where the time goes in v2:
time: 98.7 us; the launch traced here: 98.3 us
  blocking collectives  68.9 us (70%)
  starting transfers between devices  13.2 us (13%)
  local copies, waits for them, and re-layouts  7.75 us (8%)
  Pallas kernels  6.23 us (6%)
  other arithmetic  1.45 us (1%)
    all_to_all x1, blocking collectives, per_device(): got = lax.all_to_all(sent, 'pq', 0, 0, tiled=True)  41.6 us
    all_to_all x1, blocking collectives, per_device(): lax.all_to_all(jnp.broadcast_to(mine, (NZ, half, nocc)), 'pq', 0, 0, axis...  16.6 us
    all_to_all x1, blocking collectives, per_device(): parts = lax.all_to_all(fock, 'pb', 0, 0, tiled=True)  10.8 us
    ppermute x4, starting transfers between devices, per_device(): lax.ppermute(piece, 'pb', other)  9.4 us
    unnamed x10, local copies, waits for them, and re-layouts  7.74 us
    ppermute x3, starting transfers between devices, per_device(): pieces.append(lax.ppermute(near, 'pq', y_shift(k)))  3.77 us
    pallas_call x1, Pallas kernels, per_device(): pl.pallas_call(send_side, out_shape=(jax.ShapeDtypeStruct((n_dev, sent_ro...  3.77 us
    pallas_call x1, Pallas kernels, per_device(): pl.pallas_call(functools.partial(receive_side, 1.0 / (nq * n_pb)), out_sh...  2.47 us
  transfers between devices with their start and end apart: 7, of which 0 were waited for; matrix products, arithmetic and copies ran while one was open for 0% of the time, Pallas kernels for 0%

profile of v2, /device:TPU:1, one launch (start us, length us, event | category | flops | bytes accessed | tf_op | source)
XLA Modules:
  0.0 98.3 jit_solution(10722357162557072650)
XLA Ops:
  0.6 0.8 slice_select_fusion
  1.4 16.6 %all_to_all.15.near.refs_0_ = bf16[8,32,256]{2,1,0:T(8,128)(2,1)S(1)} all-to-all(bf16[8,32,256]{2,1,0:T(8,128)(2,1)S(1)} %broadcast_in_dim.3), channel_id=1, replica_groups={{0,4,8,12,16,20,24,28},{1,5,9,13,17,21,25,29},{2,6,10,14,18,22,26,30},{..., dimensions={0} | all-to-all | bytes 262144 | tf_op jit(solution)/shard_map/all_to_all | solution.py:193
  18.0 2.7 %collective-permute-start.5 = (bf16[8,32,256]{2,1,0:T(8,128)(2,1)S(1)}, bf16[8,32,256]{2,1,0:T(8,128)(2,1)S(1)}, u32[]{:S(2)}, u32[]{:S(2)}) collective-permute-start(bf16[8,32,256]{2,1,0:T(8,128)(2,1)S(1)} %all_to_all.15.near.refs_0_), channel_id=1, source_target_pairs={{0,3},{1,0},{2,1},{3,2},{4,7},{5,4},{6,5},{7,6},{8,11},{9,8},{10,9... | collective-permute-start | bytes 393224 | tf_op jit(solution)/shard_map/ppermute | solution.py:199
  20.7 0.3 collective-permute-start.3
  21.1 0.7 collective-permute-start.1
  21.8 3.1 %collective-permute-start = (bf16[8,32,256]{2,1,0:T(8,128)(2,1)S(1)}, bf16[8,32,256]{2,1,0:T(8,128)(2,1)S(1)}, u32[]{:S(2)}, u32[]{:S(2)}) collective-permute-start(bf16[8,32,256]{2,1,0:T(8,128)(2,1)S(1)} %all_to_all.15.near.refs_0_), channel_id=1, source_target_pairs={{0,32},{32,0},{64,96},{96,64},{128,160},{160,128},{192,224},{224,1... | collective-permute-start | bytes 393224 | tf_op jit(solution)/shard_map/ppermute | solution.py:200
  24.9 0.0 collective-permute-done.5.refs_6_
  24.9 2.5 %collective-permute-start.6 = (bf16[8,32,256]{2,1,0:T(8,128)(2,1)S(1)}, bf16[8,32,256]{2,1,0:T(8,128)(2,1)S(1)}, u32[]{:S(2)}, u32[]{:S(2)}) collective-permute-start(bf16[8,32,256]{2,1,0:T(8,128)(2,1)S(1)} %collective-permute-done.5.refs_6_), channel_id=1, source_target_pairs={{0,32},{32,0},{64,96},{96,64},{128,160},{160,128},{192,224},{224,1... | collective-permute-start | bytes 393224 | tf_op jit(solution)/shard_map/ppermute | solution.py:200
  27.4 0.0 collective-permute-done.3.refs_4_
  27.4 2.5 %collective-permute-start.4 = (bf16[8,32,256]{2,1,0:T(8,128)(2,1)S(1)}, bf16[8,32,256]{2,1,0:T(8,128)(2,1)S(1)}, u32[]{:S(2)}, u32[]{:S(2)}) collective-permute-start(bf16[8,32,256]{2,1,0:T(8,128)(2,1)S(1)} %collective-permute-done.3.refs_4_), channel_id=1, source_target_pairs={{0,32},{32,0},{64,96},{96,64},{128,160},{160,128},{192,224},{224,1... | collective-permute-start | bytes 393224 | tf_op jit(solution)/shard_map/ppermute | solution.py:200
  29.9 0.0 collective-permute-done.1.refs_2_
  29.9 1.3 %collective-permute-start.2 = (bf16[8,32,256]{2,1,0:T(8,128)(2,1)S(1)}, bf16[8,32,256]{2,1,0:T(8,128)(2,1)S(1)}, u32[]{:S(2)}, u32[]{:S(2)}) collective-permute-start(bf16[8,32,256]{2,1,0:T(8,128)(2,1)S(1)} %collective-permute-done.1.refs_2_), channel_id=1, source_target_pairs={{0,32},{32,0},{64,96},{96,64},{128,160},{160,128},{192,224},{224,1... | collective-permute-start | bytes 393224 | tf_op jit(solution)/shard_map/ppermute | solution.py:200
  31.2 0.0 copy-start
  31.2 3.5 %copy-done = bf16[44,56,1792]{2,1,0:T(8,128)(2,1)S(1)} copy-done((bf16[44,56,1792]{2,1,0:T(8,128)(2,1)S(1)}, bf16[44,56,1792]{2,1,0:T(8,128)(2,1)}, u32[]{:S(2)}) %copy-start) | copy-done | bytes 8831000
  34.7 0.0 copy-start.1
  34.7 1.3 %copy-done.1 = bf16[44,8,1792]{2,1,0:T(8,128)(2,1)S(1)} copy-done((bf16[44,8,1792]{2,1,0:T(8,128)(2,1)S(1)}, bf16[44,8,1792]{2,1,0:T(8,128)(2,1)}, u32[]{:S(2)}) %copy-start.1) | copy-done | bytes 1261592
  36.0 0.0 copy-start.2
  36.0 1.3 %copy-done.2 = bf16[44,256,56]{1,2,0:T(8,128)(2,1)S(1)} copy-done((bf16[44,256,56]{1,2,0:T(8,128)(2,1)S(1)}, bf16[44,256,56]{1,2,0:T(8,128)(2,1)}, u32[]{:S(2)}) %copy-start.2) | copy-done | bytes 1261592
  37.3 0.0 copy-start.3
  37.3 0.9 copy-done.3
  38.2 0.0 copy-start.4
  38.2 0.0 collective-permute-done.refs_1_
  38.2 0.0 collective-permute-done.6.refs_7_
  38.2 0.0 collective-permute-done.4.refs_5_
  38.2 0.0 collective-permute-done.2.refs_3_
  38.3 0.7 copy-done.4
  39.0 3.8 %send_side.1 = (bf16[32,184,128]{2,1,0:T(8,128)(2,1)S(1)}, bf16[1792,256]{1,0:T(8,128)(2,1)S(1)}) custom-call(f32[8,128]{1,0:T(8,128)S(1)} %touch.1.token, bf16[2464,1792]{1,0:T(8,128)(2,1)S(1)} %bitcast.6, bf16[352,1792]{1,0:T(8,128)(2,1)S(1)} %bitcast.8, bf16[44,8,256]{2,1,0:T(8,128)(2,1)S(1)} %copy-done.3, bf16[44,56,256]{2,1,0:T(8,128)(2,1)S(1)} %bitcast.10, ...), custom_call_target="tpu_custom_call" | custom-call | tf_op jit(solution)/shard_map/send_side/pallas_call | solution.py:218
  42.7 41.6 %all_to_all.16.got = bf16[32,184,128]{2,1,0:T(8,128)(2,1)S(1)} all-to-all(bf16[32,184,128]{2,1,0:T(8,128)(2,1)S(1)} %get-tuple-element.6), channel_id=1, replica_groups=mesh['pb'=8,'pq'=32] {'pq'}, dimensions={0} | all-to-all | bytes 3014656 | tf_op jit(solution)/shard_map/all_to_all | solution.py:230
  84.4 2.5 %receive_side.1 = (bf16[352,1792]{1,0:T(8,128)(2,1)}, bf16[8,8,1792]{2,1,0:T(8,128)(2,1)S(1)}) custom-call(bf16[32,184,128]{2,1,0:T(8,128)(2,1)S(1)} %all_to_all.16.got, bf16[1792,256]{1,0:T(8,128)(2,1)S(1)} %get-tuple-element.7.tt), custom_call_target="tpu_custom_call" | custom-call | tf_op jit(solution)/shard_map/receive_side/pallas_call | solution.py:232
  86.8 10.8 %all_to_all.17 = bf16[8,8,1792]{2,1,0:T(8,128)(2,1)S(1)} all-to-all(bf16[8,8,1792]{2,1,0:T(8,128)(2,1)S(1)} %get-tuple-element.9), channel_id=1, replica_groups=mesh['pb'=8,'pq'=32] {'pb'}, dimensions={0} | all-to-all | bytes 458752 | tf_op jit(solution)/shard_map/all_to_all | solution.py:244
  97.6 0.7 convert_reduce_fusion
  (2 shorter events, 0.0 us)
Async XLA Ops:
  18.0 6.9 %collective-permute-start.5 = (bf16[8,32,256]{2,1,0:T(8,128)(2,1)S(1)}, bf16[8,32,256]{2,1,0:T(8,128)(2,1)S(1)}, u32[]{:S(2)}, u32[]{:S(2)}) collective-permute-start(bf16[8,32,256]{2,1,0:T(8,128)(2,1)S(1)} %all_to_all.15.near.refs_0_), channel_id=1, source_target_pairs={{0,3},{1,0},{2,1},{3,2},{4,7},{5,4},{6,5},{7,6},{8,11},{9,8},{10,9... | collective-permute-start | bytes 393224 | tf_op jit(solution)/shard_map/ppermute | solution.py:199
  20.7 6.7 %collective-permute-start.3 = (bf16[8,32,256]{2,1,0:T(8,128)(2,1)S(1)}, bf16[8,32,256]{2,1,0:T(8,128)(2,1)S(1)}, u32[]{:S(2)}, u32[]{:S(2)}) collective-permute-start(bf16[8,32,256]{2,1,0:T(8,128)(2,1)S(1)} %all_to_all.15.near.refs_0_), channel_id=1, source_target_pairs={{0,2},{1,3},{2,0},{3,1},{4,6},{5,7},{6,4},{7,5},{8,10},{9,11},{10,... | collective-permute-start | bytes 393224 | tf_op jit(solution)/shard_map/ppermute | solution.py:199
  21.1 8.8 %collective-permute-start.1 = (bf16[8,32,256]{2,1,0:T(8,128)(2,1)S(1)}, bf16[8,32,256]{2,1,0:T(8,128)(2,1)S(1)}, u32[]{:S(2)}, u32[]{:S(2)}) collective-permute-start(bf16[8,32,256]{2,1,0:T(8,128)(2,1)S(1)} %all_to_all.15.near.refs_0_), channel_id=1, source_target_pairs={{0,1},{1,2},{2,3},{3,0},{4,5},{5,6},{6,7},{7,4},{8,9},{9,10},{10,1... | collective-permute-start | bytes 393224 | tf_op jit(solution)/shard_map/ppermute | solution.py:199
  21.8 16.4 %collective-permute-start = (bf16[8,32,256]{2,1,0:T(8,128)(2,1)S(1)}, bf16[8,32,256]{2,1,0:T(8,128)(2,1)S(1)}, u32[]{:S(2)}, u32[]{:S(2)}) collective-permute-start(bf16[8,32,256]{2,1,0:T(8,128)(2,1)S(1)} %all_to_all.15.near.refs_0_), channel_id=1, source_target_pairs={{0,32},{32,0},{64,96},{96,64},{128,160},{160,128},{192,224},{224,1... | collective-permute-start | bytes 393224 | tf_op jit(solution)/shard_map/ppermute | solution.py:200
  24.9 13.3 %collective-permute-start.6 = (bf16[8,32,256]{2,1,0:T(8,128)(2,1)S(1)}, bf16[8,32,256]{2,1,0:T(8,128)(2,1)S(1)}, u32[]{:S(2)}, u32[]{:S(2)}) collective-permute-start(bf16[8,32,256]{2,1,0:T(8,128)(2,1)S(1)} %collective-permute-done.5.refs_6_), channel_id=1, source_target_pairs={{0,32},{32,0},{64,96},{96,64},{128,160},{160,128},{192,224},{224,1... | collective-permute-start | bytes 393224 | tf_op jit(solution)/shard_map/ppermute | solution.py:200
  27.4 10.8 %collective-permute-start.4 = (bf16[8,32,256]{2,1,0:T(8,128)(2,1)S(1)}, bf16[8,32,256]{2,1,0:T(8,128)(2,1)S(1)}, u32[]{:S(2)}, u32[]{:S(2)}) collective-permute-start(bf16[8,32,256]{2,1,0:T(8,128)(2,1)S(1)} %collective-permute-done.3.refs_4_), channel_id=1, source_target_pairs={{0,32},{32,0},{64,96},{96,64},{128,160},{160,128},{192,224},{224,1... | collective-permute-start | bytes 393224 | tf_op jit(solution)/shard_map/ppermute | solution.py:200
  29.9 8.4 %collective-permute-start.2 = (bf16[8,32,256]{2,1,0:T(8,128)(2,1)S(1)}, bf16[8,32,256]{2,1,0:T(8,128)(2,1)S(1)}, u32[]{:S(2)}, u32[]{:S(2)}) collective-permute-start(bf16[8,32,256]{2,1,0:T(8,128)(2,1)S(1)} %collective-permute-done.1.refs_2_), channel_id=1, source_target_pairs={{0,32},{32,0},{64,96},{96,64},{128,160},{160,128},{192,224},{224,1... | collective-permute-start | bytes 393224 | tf_op jit(solution)/shard_map/ppermute | solution.py:200
  31.2 3.5 %copy-start = (bf16[44,56,1792]{2,1,0:T(8,128)(2,1)S(1)}, bf16[44,56,1792]{2,1,0:T(8,128)(2,1)}, u32[]{:S(2)}) copy-start(bf16[44,56,1792]{2,1,0:T(8,128)(2,1)} %param.5) | copy-start | bytes 26492932
  34.7 1.3 %copy-start.1 = (bf16[44,8,1792]{2,1,0:T(8,128)(2,1)S(1)}, bf16[44,8,1792]{2,1,0:T(8,128)(2,1)}, u32[]{:S(2)}) copy-start(bf16[44,8,1792]{2,1,0:T(8,128)(2,1)} %param.6) | copy-start | bytes 3784708
  36.0 1.3 %copy-start.2 = (bf16[44,256,56]{1,2,0:T(8,128)(2,1)S(1)}, bf16[44,256,56]{1,2,0:T(8,128)(2,1)}, u32[]{:S(2)}) copy-start(bf16[44,256,56]{1,2,0:T(8,128)(2,1)} %param.8) | copy-start | bytes 3784708
  37.3 0.9 copy-start.3
  38.2 0.7 copy-start.4

commit v3 on v2

--- a/solution.py
+++ b/solution.py
@@ -47,6 +47,14 @@
         tiles = out
         bit *= 2
     return tiles
+
+
+def spread(own, out):
+    half = out.shape[1]
+    start = (lax.axis_index("pb") & 1) * (own.shape[0] - half)
+    part = own[pl.ds(pl.multiple_of(start, 8), half), :]
+    for copy in range(out.shape[0]):
+        out[copy] = part
 
 
 def touch(near, vv, ov, oo, vo, token):
@@ -179,6 +187,7 @@
 
 VMEM = pl.BlockSpec(memory_space=pltpu.VMEM)
 ANY = pl.BlockSpec(memory_space=pl.ANY)
+FLOPS = 40_000_000_000
 PARAMS = pltpu.CompilerParams(vmem_limit_bytes=26 * 1024 * 1024)
 
 
@@ -188,11 +197,16 @@
     n_dev, n_pb = lax.axis_size("pq"), lax.axis_size("pb")
     own = amplitudes.T
     half = -(-n_own // 16) * 8
-    core = lax.axis_index("pb") & 1
-    mine = jnp.where(core == 0, own[:half], own[n_own - half :])
-    near = lax.all_to_all(
-        jnp.broadcast_to(mine, (NZ, half, nocc)), "pq", 0, 0, axis_index_groups=z_groups(), tiled=True
-    )
+    copies = pl.pallas_call(
+        spread,
+        out_shape=jax.ShapeDtypeStruct((NZ, half, nocc), BF16),
+        in_specs=[VMEM],
+        out_specs=VMEM,
+        compiler_params=PARAMS,
+        cost_estimate=pl.CostEstimate(flops=FLOPS, bytes_accessed=0, transcendentals=0),
+        name="spread",
+    )(own)
+    near = lax.all_to_all(copies, "pq", 0, 0, axis_index_groups=z_groups(), tiled=True)
     other = [(b, b ^ 1) for b in range(n_pb)]
     pieces = [near]
     for k in range(1, NY):
@@ -256,4 +270,6 @@
     )
     out_specs = (P("pb", "pq", None), P("pq", None))
 
-    return jax.shard_map(per_device, mesh=mesh, in_specs=in_specs, out_specs=out_specs, check_vma=False)
+    return jax.shard_map(
+        per_device, mesh=mesh, in_specs=in_specs, out_specs=out_specs, check_vma=False
+    )

time: 98.7 us -> 92.4 us (0.936)
  local copies, waits for them, and re-layouts: 7.75 us -> 0.76 us
    unnamed x10, local copies, waits for them, and re-layouts: 7.74 us -> 0.76 us
  transfers between devices with their start and end apart: 7 -> 7, of which waited for: 0 -> 1; matrix products, arithmetic and copies ran while one was open for 0% -> 0% of each run, Pallas kernels for 0% -> 0%
where the time goes in v3:
time: 92.4 us; the launch traced here: 92.1 us
  blocking collectives  69.6 us (75%)
  starting transfers between devices  13.2 us (14%)
  Pallas kernels  6.32 us (7%)
  waiting for transfers between devices  0.95 us (1%)
    all_to_all x1, blocking collectives, per_device(): got = lax.all_to_all(sent, 'pq', 0, 0, tiled=True)  41.3 us
    all_to_all x1, blocking collectives, per_device(): lax.all_to_all(copies, 'pq', 0, 0, axis_index_groups=z_groups(), tiled=True)  16.8 us
    all_to_all x1, blocking collectives, per_device(): parts = lax.all_to_all(fock, 'pb', 0, 0, tiled=True)  11.5 us
    ppermute x4, starting transfers between devices, per_device(): lax.ppermute(piece, 'pb', other)  9.4 us
    pallas_call x1, Pallas kernels, per_device(): pl.pallas_call(send_side, out_shape=(jax.ShapeDtypeStruct((n_dev, sent_ro...  3.82 us
    ppermute x3, starting transfers between devices, per_device(): pieces.append(lax.ppermute(near, 'pq', y_shift(k)))  3.77 us
    pallas_call x1, Pallas kernels, per_device(): pl.pallas_call(functools.partial(receive_side, 1.0 / (nq * n_pb)), out_sh...  2.47 us
  transfers between devices with their start and end apart: 7, of which 1 were waited for; matrix products, arithmetic and copies ran while one was open for 0% of the time, Pallas kernels for 0%

profile of v3, /device:TPU:1, one launch (start us, length us, event | category | flops | bytes accessed | tf_op | source)
XLA Modules:
  0.0 92.1 jit_solution(2075953408471684533)
XLA Ops:
  0.6 0.0 copy-start.4
  0.6 0.7 copy-done.4
  1.4 0.0 copy-start
  1.4 0.0 copy-start.1
  1.4 0.0 copy-start.2
  1.4 0.0 copy-start.3
  1.4 16.8 %all_to_all.15.near.refs_0_ = bf16[8,32,256]{2,1,0:T(8,128)(2,1)S(1)} all-to-all(bf16[8,32,256]{2,1,0:T(8,128)(2,1)S(1)} %spread.1), channel_id=1, replica_groups={{0,4,8,12,16,20,24,28},{1,5,9,13,17,21,25,29},{2,6,10,14,18,22,26,30},{..., dimensions={0} | all-to-all | bytes 262144 | tf_op jit(solution)/shard_map/all_to_all | solution.py:209
  18.2 2.7 %collective-permute-start.5 = (bf16[8,32,256]{2,1,0:T(8,128)(2,1)S(1)}, bf16[8,32,256]{2,1,0:T(8,128)(2,1)S(1)}, u32[]{:S(2)}, u32[]{:S(2)}) collective-permute-start(bf16[8,32,256]{2,1,0:T(8,128)(2,1)S(1)} %all_to_all.15.near.refs_0_), channel_id=1, source_target_pairs={{0,3},{1,0},{2,1},{3,2},{4,7},{5,4},{6,5},{7,6},{8,11},{9,8},{10,9... | collective-permute-start | bytes 393224 | tf_op jit(solution)/shard_map/ppermute | solution.py:213
  21.0 0.3 collective-permute-start.3
  21.3 0.7 collective-permute-start.1
  22.0 3.1 %collective-permute-start = (bf16[8,32,256]{2,1,0:T(8,128)(2,1)S(1)}, bf16[8,32,256]{2,1,0:T(8,128)(2,1)S(1)}, u32[]{:S(2)}, u32[]{:S(2)}) collective-permute-start(bf16[8,32,256]{2,1,0:T(8,128)(2,1)S(1)} %all_to_all.15.near.refs_0_), channel_id=1, source_target_pairs={{0,32},{32,0},{64,96},{96,64},{128,160},{160,128},{192,224},{224,1... | collective-permute-start | bytes 393224 | tf_op jit(solution)/shard_map/ppermute | solution.py:214
  25.2 0.0 collective-permute-done.5.refs_6_
  25.2 2.5 %collective-permute-start.6 = (bf16[8,32,256]{2,1,0:T(8,128)(2,1)S(1)}, bf16[8,32,256]{2,1,0:T(8,128)(2,1)S(1)}, u32[]{:S(2)}, u32[]{:S(2)}) collective-permute-start(bf16[8,32,256]{2,1,0:T(8,128)(2,1)S(1)} %collective-permute-done.5.refs_6_), channel_id=1, source_target_pairs={{0,32},{32,0},{64,96},{96,64},{128,160},{160,128},{192,224},{224,1... | collective-permute-start | bytes 393224 | tf_op jit(solution)/shard_map/ppermute | solution.py:214
  27.7 0.0 collective-permute-done.3.refs_4_
  27.7 2.5 %collective-permute-start.4 = (bf16[8,32,256]{2,1,0:T(8,128)(2,1)S(1)}, bf16[8,32,256]{2,1,0:T(8,128)(2,1)S(1)}, u32[]{:S(2)}, u32[]{:S(2)}) collective-permute-start(bf16[8,32,256]{2,1,0:T(8,128)(2,1)S(1)} %collective-permute-done.3.refs_4_), channel_id=1, source_target_pairs={{0,32},{32,0},{64,96},{96,64},{128,160},{160,128},{192,224},{224,1... | collective-permute-start | bytes 393224 | tf_op jit(solution)/shard_map/ppermute | solution.py:214
  30.1 0.0 collective-permute-done.1.refs_2_
  30.1 1.3 %collective-permute-start.2 = (bf16[8,32,256]{2,1,0:T(8,128)(2,1)S(1)}, bf16[8,32,256]{2,1,0:T(8,128)(2,1)S(1)}, u32[]{:S(2)}, u32[]{:S(2)}) collective-permute-start(bf16[8,32,256]{2,1,0:T(8,128)(2,1)S(1)} %collective-permute-done.1.refs_2_), channel_id=1, source_target_pairs={{0,32},{32,0},{64,96},{96,64},{128,160},{160,128},{192,224},{224,1... | collective-permute-start | bytes 393224 | tf_op jit(solution)/shard_map/ppermute | solution.py:214
  31.4 0.0 copy-done
  31.4 0.0 copy-done.1
  31.4 0.0 copy-done.2
  31.4 0.0 copy-done.3
  31.5 0.0 collective-permute-done.refs_1_
  31.5 0.0 collective-permute-done.6.refs_7_
  31.5 0.0 collective-permute-done.4.refs_5_
  31.5 0.9 %collective-permute-done.2.refs_3_ = bf16[8,32,256]{2,1,0:T(8,128)(2,1)S(1)} collective-permute-done((bf16[8,32,256]{2,1,0:T(8,128)(2,1)S(1)}, bf16[8,32,256]{2,1,0:T(8,128)(2,1)S(1)}, u32[]{:S(2)}, u32[]{:S(2)}) %collective-permute-start.2) | collective-permute-done | bytes 131104 | tf_op jit(solution)/shard_map/ppermute | solution.py:214
  32.4 3.8 %send_side.1 = (bf16[32,184,128]{2,1,0:T(8,128)(2,1)S(1)}, bf16[1792,256]{1,0:T(8,128)(2,1)S(1)}) custom-call(f32[8,128]{1,0:T(8,128)S(1)} %touch.1.token, bf16[2464,1792]{1,0:T(8,128)(2,1)S(1)} %bitcast.6, bf16[352,1792]{1,0:T(8,128)(2,1)S(1)} %bitcast.8, bf16[44,8,256]{2,1,0:T(8,128)(2,1)S(1)} %copy-done.3, bf16[44,56,256]{2,1,0:T(8,128)(2,1)S(1)} %bitcast.10, ...), custom_call_target="tpu_custom_call" | custom-call | tf_op jit(solution)/shard_map/send_side/pallas_call | solution.py:232
  36.2 41.3 %all_to_all.16.got = bf16[32,184,128]{2,1,0:T(8,128)(2,1)S(1)} all-to-all(bf16[32,184,128]{2,1,0:T(8,128)(2,1)S(1)} %get-tuple-element.6), channel_id=1, replica_groups=mesh['pb'=8,'pq'=32] {'pq'}, dimensions={0} | all-to-all | bytes 3014656 | tf_op jit(solution)/shard_map/all_to_all | solution.py:244
  77.5 2.5 %receive_side.1 = (bf16[352,1792]{1,0:T(8,128)(2,1)}, bf16[8,8,1792]{2,1,0:T(8,128)(2,1)S(1)}) custom-call(bf16[32,184,128]{2,1,0:T(8,128)(2,1)S(1)} %all_to_all.16.got, bf16[1792,256]{1,0:T(8,128)(2,1)S(1)} %get-tuple-element.7.tt), custom_call_target="tpu_custom_call" | custom-call | tf_op jit(solution)/shard_map/receive_side/pallas_call | solution.py:246
  80.0 11.5 %all_to_all.17 = bf16[8,8,1792]{2,1,0:T(8,128)(2,1)S(1)} all-to-all(bf16[8,8,1792]{2,1,0:T(8,128)(2,1)S(1)} %get-tuple-element.9), channel_id=1, replica_groups=mesh['pb'=8,'pq'=32] {'pb'}, dimensions={0} | all-to-all | bytes 458752 | tf_op jit(solution)/shard_map/all_to_all | solution.py:258
  91.5 0.7 convert_reduce_fusion
  (2 shorter events, 0.0 us)
Async XLA Ops:
  0.6 0.7 copy-start.4
  1.4 30.1 %copy-start = (bf16[44,56,1792]{2,1,0:T(8,128)(2,1)S(1)}, bf16[44,56,1792]{2,1,0:T(8,128)(2,1)}, u32[]{:S(2)}) copy-start(bf16[44,56,1792]{2,1,0:T(8,128)(2,1)} %param.5) | copy-start | bytes 26492932
  1.4 30.1 %copy-start.1 = (bf16[44,8,1792]{2,1,0:T(8,128)(2,1)S(1)}, bf16[44,8,1792]{2,1,0:T(8,128)(2,1)}, u32[]{:S(2)}) copy-start(bf16[44,8,1792]{2,1,0:T(8,128)(2,1)} %param.6) | copy-start | bytes 3784708
  1.4 30.1 %copy-start.2 = (bf16[44,256,56]{1,2,0:T(8,128)(2,1)S(1)}, bf16[44,256,56]{1,2,0:T(8,128)(2,1)}, u32[]{:S(2)}) copy-start(bf16[44,256,56]{1,2,0:T(8,128)(2,1)} %param.8) | copy-start | bytes 3784708
  1.4 30.1 %copy-start.3 = (bf16[44,8,256]{2,1,0:T(8,128)(2,1)S(1)}, bf16[44,8,256]{2,1,0:T(8,128)(2,1)}, u32[]{:S(2)}) copy-start(bf16[44,8,256]{2,1,0:T(8,128)(2,1)} %oo.3) | copy-start | bytes 540676
  18.2 6.9 %collective-permute-start.5 = (bf16[8,32,256]{2,1,0:T(8,128)(2,1)S(1)}, bf16[8,32,256]{2,1,0:T(8,128)(2,1)S(1)}, u32[]{:S(2)}, u32[]{:S(2)}) collective-permute-start(bf16[8,32,256]{2,1,0:T(8,128)(2,1)S(1)} %all_to_all.15.near.refs_0_), channel_id=1, source_target_pairs={{0,3},{1,0},{2,1},{3,2},{4,7},{5,4},{6,5},{7,6},{8,11},{9,8},{10,9... | collective-permute-start | bytes 393224 | tf_op jit(solution)/shard_map/ppermute | solution.py:213
  21.0 6.7 %collective-permute-start.3 = (bf16[8,32,256]{2,1,0:T(8,128)(2,1)S(1)}, bf16[8,32,256]{2,1,0:T(8,128)(2,1)S(1)}, u32[]{:S(2)}, u32[]{:S(2)}) collective-permute-start(bf16[8,32,256]{2,1,0:T(8,128)(2,1)S(1)} %all_to_all.15.near.refs_0_), channel_id=1, source_target_pairs={{0,2},{1,3},{2,0},{3,1},{4,6},{5,7},{6,4},{7,5},{8,10},{9,11},{10,... | collective-permute-start | bytes 393224 | tf_op jit(solution)/shard_map/ppermute | solution.py:213
  21.3 8.8 %collective-permute-start.1 = (bf16[8,32,256]{2,1,0:T(8,128)(2,1)S(1)}, bf16[8,32,256]{2,1,0:T(8,128)(2,1)S(1)}, u32[]{:S(2)}, u32[]{:S(2)}) collective-permute-start(bf16[8,32,256]{2,1,0:T(8,128)(2,1)S(1)} %all_to_all.15.near.refs_0_), channel_id=1, source_target_pairs={{0,1},{1,2},{2,3},{3,0},{4,5},{5,6},{6,7},{7,4},{8,9},{9,10},{10,1... | collective-permute-start | bytes 393224 | tf_op jit(solution)/shard_map/ppermute | solution.py:213
  22.0 9.4 %collective-permute-start = (bf16[8,32,256]{2,1,0:T(8,128)(2,1)S(1)}, bf16[8,32,256]{2,1,0:T(8,128)(2,1)S(1)}, u32[]{:S(2)}, u32[]{:S(2)}) collective-permute-start(bf16[8,32,256]{2,1,0:T(8,128)(2,1)S(1)} %all_to_all.15.near.refs_0_), channel_id=1, source_target_pairs={{0,32},{32,0},{64,96},{96,64},{128,160},{160,128},{192,224},{224,1... | collective-permute-start | bytes 393224 | tf_op jit(solution)/shard_map/ppermute | solution.py:214
  25.2 6.3 %collective-permute-start.6 = (bf16[8,32,256]{2,1,0:T(8,128)(2,1)S(1)}, bf16[8,32,256]{2,1,0:T(8,128)(2,1)S(1)}, u32[]{:S(2)}, u32[]{:S(2)}) collective-permute-start(bf16[8,32,256]{2,1,0:T(8,128)(2,1)S(1)} %collective-permute-done.5.refs_6_), channel_id=1, source_target_pairs={{0,32},{32,0},{64,96},{96,64},{128,160},{160,128},{192,224},{224,1... | collective-permute-start | bytes 393224 | tf_op jit(solution)/shard_map/ppermute | solution.py:214
  27.7 3.8 %collective-permute-start.4 = (bf16[8,32,256]{2,1,0:T(8,128)(2,1)S(1)}, bf16[8,32,256]{2,1,0:T(8,128)(2,1)S(1)}, u32[]{:S(2)}, u32[]{:S(2)}) collective-permute-start(bf16[8,32,256]{2,1,0:T(8,128)(2,1)S(1)} %collective-permute-done.3.refs_4_), channel_id=1, source_target_pairs={{0,32},{32,0},{64,96},{96,64},{128,160},{160,128},{192,224},{224,1... | collective-permute-start | bytes 393224 | tf_op jit(solution)/shard_map/ppermute | solution.py:214
  30.1 2.3 %collective-permute-start.2 = (bf16[8,32,256]{2,1,0:T(8,128)(2,1)S(1)}, bf16[8,32,256]{2,1,0:T(8,128)(2,1)S(1)}, u32[]{:S(2)}, u32[]{:S(2)}) collective-permute-start(bf16[8,32,256]{2,1,0:T(8,128)(2,1)S(1)} %collective-permute-done.1.refs_2_), channel_id=1, source_target_pairs={{0,32},{32,0},{64,96},{96,64},{128,160},{160,128},{192,224},{224,1... | collective-permute-start | bytes 393224 | tf_op jit(solution)/shard_map/ppermute | solution.py:214

commit v4 on v3

--- a/solution.py
+++ b/solution.py
@@ -14,6 +14,10 @@
 F32, BF16 = jnp.float32, jnp.bfloat16
 NT = (((1,), (1,)), ((), ()))
 TN = (((0,), (0,)), ((), ()))
+
+
+ORDER = [z * NY + y for y in range(NY) for z in range(NZ)]
+PLACE = [ORDER.index(p) for p in range(NZ * NY)]
 
 
 def z_groups():
@@ -50,9 +54,8 @@
 
 
 def spread(own, out):
-    half = out.shape[1]
-    start = (lax.axis_index("pb") & 1) * (own.shape[0] - half)
-    part = own[pl.ds(pl.multiple_of(start, 8), half), :]
+    start = pl.multiple_of((lax.axis_index("pb") & 1) * LANES, LANES)
+    part = own[:, pl.ds(start, LANES)]
     for copy in range(out.shape[0]):
         out[copy] = part
 
@@ -71,14 +74,13 @@
     me = lax.axis_index("pq")
     core = lax.axis_index("pb") & 1
     y = me & (NY - 1)
-    half = pieces[0].shape[1]
     for k in range(NY):
         src = (y - k + NY) & (NY - 1)
         for c in range(2):
-            shift = (core if c == 0 else 1 - core) * (n_own - half)
+            cols = pl.multiple_of((core if c == 0 else 1 - core) * LANES, LANES)
             for z in range(NZ):
-                at = pl.multiple_of((z * NY + src) * n_own + shift, 8)
-                tt[pl.ds(at, half), :] = pieces[2 * k + c][z]
+                at = pl.multiple_of((z * NY + src) * n_own, 8)
+                tt[pl.ds(at, n_own), pl.ds(cols, LANES)] = pieces[2 * k + c][z]
     amps = tt[...]
     lp = jnp.dot(ov[...], amps, preferred_element_type=F32).reshape(nq, OWN_I, nocc)
     d[:, n_own:, :] = (lp + oo[...].astype(F32)).astype(BF16).astype(F32)
@@ -106,7 +108,7 @@
                         for v in range(spare)
                     ]
                 for g, tile in enumerate(swap_blocks(tiles)):
-                    out[h * GROUP + g, t * rows + r : t * rows + r + 8, :] = tile.astype(BF16)
+                    out[PLACE[h * GROUP + g], t * rows + r : t * rows + r + 8, :] = tile.astype(BF16)
 
     lane = lax.broadcasted_iota(jnp.int32, (1, LANES), 1)
     row = jnp.zeros((1, LANES), F32)
@@ -131,12 +133,12 @@
         out[p, at : at + 8, :] = block
 
 
-def receive_side(scale, got, tt, dressed, fock, raw, lpt):
+def unpack(scale, got, tt, fock, raw, lpt):
     n_dev = got.shape[0]
-    nq = dressed.shape[0] // OWN_I
     nvirt = tt.shape[0]
     n_own = nvirt // n_dev
     rows = n_own + OWN_I
+    nq = (got.shape[1] - 8) * LANES // OWN_I // rows
     full = nq // GROUP * GROUP
     n_full = full // GROUP
     left = nq - full
@@ -145,44 +147,66 @@
     lane16 = lax.broadcasted_iota(jnp.int32, (16, LANES), 1)
     width = spare * OWN_I
     for p in range(n_dev):
-        a = p * n_own
+        a, k = p * n_own, PLACE[p]
         for t in range(n_full):
-            raw[a : a + n_own, t * LANES : (t + 1) * LANES] = got[p, t * rows : t * rows + n_own, :]
+            raw[a : a + n_own, t * LANES : (t + 1) * LANES] = got[k, t * rows : t * rows + n_own, :]
             lpt[p * OWN_I : (p + 1) * OWN_I, t * LANES : (t + 1) * LANES] = got[
-                p, t * rows + n_own : (t + 1) * rows, :
+                k, t * rows + n_own : (t + 1) * rows, :
             ]
         base = n_full * rows
         tail = jnp.zeros((16, LANES), F32)
         for n in range(short // 16):
             part = pltpu.roll(
-                got[p, base + 16 * n : base + 16 * (n + 1), :].astype(F32), (n + 1) * width, 1
+                got[k, base + 16 * n : base + 16 * (n + 1), :].astype(F32), (n + 1) * width, 1
             )
             here = (lane16 >= n * width) & (lane16 < (n + 1) * width)
             tail = jnp.where(here, part, tail)
-        raw[a : a + short, n_full * LANES :] = got[p, base : base + short, :]
+        raw[a : a + short, n_full * LANES :] = got[k, base : base + short, :]
         raw[a + short : a + n_own, n_full * LANES :] = tail[: n_own - short].astype(BF16)
         lpt[p * OWN_I : (p + 1) * OWN_I, n_full * LANES :] = tail[n_own - short :].astype(BF16)
     lanes_in = (n_full + 1) * LANES
-    m = nq * OWN_I
+    at = n_full * rows + short
+    shares = jnp.sum(got[:, at : at + 8, :].astype(F32), axis=0)
+    coulomb = jnp.broadcast_to((shares[0:1] + shares[1:2] + shares[2:3]) * scale, (OWN_I, LANES))
+    column = lax.broadcasted_iota(jnp.int32, (LANES, lanes_in), 1)
+    widen = (lax.broadcasted_iota(jnp.int32, (LANES, lanes_in), 0) == column // OWN_I).astype(F32).astype(BF16)
+    column = lax.broadcasted_iota(jnp.int32, (OWN_I, lanes_in), 1)
+    own_row = (column % OWN_I == lax.broadcasted_iota(jnp.int32, (OWN_I, lanes_in), 0)) & (
+        column < nq * OWN_I
+    )
+    weight = jnp.concatenate(
+        [
+            jnp.where(own_row, jnp.dot(part, widen, preferred_element_type=F32), 0.0)
+            for part in split3(coulomb)
+        ],
+        0,
+    ).astype(BF16)
+
+    def three(x):
+        return x[:OWN_I] + x[OWN_I : 2 * OWN_I] + x[2 * OWN_I :]
+
+    moved = three(lax.dot_general(weight, raw[...], NT, preferred_element_type=F32))
+    lp = three(lax.dot_general(weight, lpt[...], NT, preferred_element_type=F32))
+    lp = jnp.concatenate([part.astype(F32) for part in split3(lp)], 0).astype(BF16)
+    part = moved - three(lax.dot_general(lp, tt[...], NT, preferred_element_type=F32))
+    fock[...] = part
+
+
+def both_cores(own, other, out):
+    total = (own[...] + other[...]).astype(out.dtype)
+    for copy in range(out.shape[0]):
+        out[copy] = total
+
+
+def dress(raw, lpt, tt, dressed):
+    shape = (dressed.shape[0], raw.shape[1])
     eye = (
-        lax.broadcasted_iota(jnp.int32, (m, lanes_in), 0)
-        == lax.broadcasted_iota(jnp.int32, (m, lanes_in), 1)
+        lax.broadcasted_iota(jnp.int32, shape, 0) == lax.broadcasted_iota(jnp.int32, shape, 1)
     ).astype(F32).astype(BF16)
     lp = lax.dot_general(eye, lpt[...], NT, preferred_element_type=F32).astype(BF16)
     moved = lax.dot_general(eye, raw[...], NT, preferred_element_type=F32)
     occupied = lax.dot_general(lp, tt[...], NT, preferred_element_type=F32)
-    result = (moved - occupied).astype(BF16)
-    dressed[...] = result
-    at = n_full * rows + short
-    shares = jnp.sum(got[:, at : at + 8, :].astype(F32), axis=0)
-    coulomb = shares[0:1] + shares[1:2] + shares[2:3]
-    pick = lax.broadcasted_iota(jnp.int32, (m, LANES), 1) == lax.broadcasted_iota(
-        jnp.int32, (m, LANES), 0
-    ) // OWN_I
-    column = jnp.sum(jnp.where(pick, coulomb, 0.0), axis=1, keepdims=True)
-    part = jnp.sum((column * result.astype(F32)).reshape(nq, OWN_I, nvirt), axis=0) * scale
-    for copy in range(fock.shape[0]):
-        fock[copy] = part.astype(fock.dtype)
+    dressed[...] = (moved - occupied).astype(BF16)
 
 
 VMEM = pl.BlockSpec(memory_space=pltpu.VMEM)
@@ -196,10 +220,9 @@
     nocc = amplitudes.shape[0]
     n_dev, n_pb = lax.axis_size("pq"), lax.axis_size("pb")
     own = amplitudes.T
-    half = -(-n_own // 16) * 8
     copies = pl.pallas_call(
         spread,
-        out_shape=jax.ShapeDtypeStruct((NZ, half, nocc), BF16),
+        out_shape=jax.ShapeDtypeStruct((NZ, n_own, LANES), BF16),
         in_specs=[VMEM],
         out_specs=VMEM,
         compiler_params=PARAMS,
@@ -241,21 +264,40 @@
         compiler_params=PARAMS,
         name="send_side",
     )(token, *blocks, own, *pieces)
-    got = lax.all_to_all(sent, "pq", 0, 0, tiled=True)
+    got = lax.all_to_all(sent, "pq", 0, 0, axis_index_groups=[ORDER], tiled=True)
     lanes_in = -(-nq // GROUP) * LANES
-    dressed, fock = pl.pallas_call(
-        functools.partial(receive_side, 1.0 / (nq * n_pb)),
+    fock, raw, lpt = pl.pallas_call(
+        functools.partial(unpack, 1.0 / (nq * n_pb)),
         out_shape=(
-            jax.ShapeDtypeStruct((nq * OWN_I, nvirt), BF16),
-            jax.ShapeDtypeStruct((n_pb, OWN_I, nvirt), BF16),
+            jax.ShapeDtypeStruct((OWN_I, nvirt), F32),
+            jax.ShapeDtypeStruct((nvirt, lanes_in), BF16),
+            jax.ShapeDtypeStruct((nocc, lanes_in), BF16),
         ),
         in_specs=[VMEM] * 2,
-        out_specs=(VMEM, VMEM),
-        scratch_shapes=[pltpu.VMEM((nvirt, lanes_in), BF16), pltpu.VMEM((nocc, lanes_in), BF16)],
-        compiler_params=PARAMS,
-        name="receive_side",
+        out_specs=(VMEM,) * 3,
+        compiler_params=PARAMS,
+        name="unpack",
     )(got, tt)
-    parts = lax.all_to_all(fock, "pb", 0, 0, tiled=True)
+    dressed = pl.pallas_call(
+        dress,
+        out_shape=jax.ShapeDtypeStruct((nq * OWN_I, nvirt), BF16),
+        in_specs=[VMEM] * 3,
+        out_specs=VMEM,
+        compiler_params=PARAMS,
+        cost_estimate=pl.CostEstimate(flops=FLOPS, bytes_accessed=0, transcendentals=0),
+        name="dress",
+    )(raw, lpt, tt)
+    partner = lax.ppermute(fock, "pb", other)
+    halves = pl.pallas_call(
+        both_cores,
+        out_shape=jax.ShapeDtypeStruct((n_pb // 2, OWN_I, nvirt), BF16),
+        in_specs=[VMEM] * 2,
+        out_specs=VMEM,
+        compiler_params=PARAMS,
+        name="both_cores",
+    )(fock, partner)
+    x_groups = [list(range(c, n_pb, 2)) for c in range(2)]
+    parts = lax.all_to_all(halves, "pb", 0, 0, axis_index_groups=x_groups, tiled=True)
     fock_ov = jnp.sum(parts.astype(F32), axis=0)
     return dressed.reshape(nq, OWN_I, nvirt), fock_ov
 
@@ -270,6 +312,4 @@
     )
     out_specs = (P("pb", "pq", None), P("pq", None))
 
-    return jax.shard_map(
-        per_device, mesh=mesh, in_specs=in_specs, out_specs=out_specs, check_vma=False
-    )
+    return jax.shard_map(per_device, mesh=mesh, in_specs=in_specs, out_specs=out_specs, check_vma=False)

time: 92.4 us -> 90.9 us (0.984); the launches traced: 92.1 us -> 89.6 us
  blocking collectives: 69.6 us -> 55.7 us
  starting transfers between devices: 13.2 us -> 19.7 us
  waiting for transfers between devices: 0.95 us -> 4.24 us
  Pallas kernels: 6.32 us -> 7.92 us
    all_to_all x2 -> x1, blocking collectives: 52.8 us -> 39 us  [per_device(): lax.all_to_all(sent, 'pq', 0, 0, axis_index_groups=[ORDER], tiled=True)]
    all_to_all x0 -> x1, starting transfers between devices: none -> 3.99 us  [per_device(): lax.all_to_all(halves, 'pb', 0, 0, axis_index_groups=x_groups, tiled=True)]
    ppermute x0 -> x1, starting transfers between devices: none -> 2.92 us  [per_device(): partner = lax.ppermute(fock, 'pb', other)]
    all_to_all x0 -> x1, waiting for transfers between devices: none -> 2.43 us  [per_device(): lax.all_to_all(halves, 'pb', 0, 0, axis_index_groups=x_groups, tiled=True)]
    pallas_call x2 -> x4, Pallas kernels: 2.49 us -> 4.08 us  [the longest x1 2.31 us: per_device(): pl.pallas_call(dress, out_shape=jax.ShapeDtypeStruct((nq * OWN_I, nvirt),...]
  transfers between devices with their start and end apart: 7 -> 9, of which waited for: 1 -> 3; matrix products, arithmetic and copies ran while one was open for 0% -> 0% of each run, Pallas kernels for 0% -> 3%
where the time goes in v4:
time: 90.9 us; the launch traced here: 89.6 us
  blocking collectives  55.7 us (61%)
  starting transfers between devices  19.7 us (22%)
  Pallas kernels  7.92 us (9%)
  waiting for transfers between devices  4.24 us (5%)
    all_to_all x1, blocking collectives, per_device(): lax.all_to_all(sent, 'pq', 0, 0, axis_index_groups=[ORDER], tiled=True)  39 us
    all_to_all x1, blocking collectives, per_device(): lax.all_to_all(copies, 'pq', 0, 0, axis_index_groups=z_groups(), tiled=True)  16.7 us
    ppermute x4, starting transfers between devices, per_device(): lax.ppermute(piece, 'pb', other)  9.01 us
    all_to_all x1, starting transfers between devices, per_device(): lax.all_to_all(halves, 'pb', 0, 0, axis_index_groups=x_groups, tiled=True)  3.99 us
    pallas_call x1, Pallas kernels, per_device(): pl.pallas_call(send_side, out_shape=(jax.ShapeDtypeStruct((n_dev, sent_ro...  3.84 us
    ppermute x3, starting transfers between devices, per_device(): pieces.append(lax.ppermute(near, 'pq', y_shift(k)))  3.77 us
    ppermute x1, starting transfers between devices, per_device(): partner = lax.ppermute(fock, 'pb', other)  2.92 us
    all_to_all x1, waiting for transfers between devices, per_device(): lax.all_to_all(halves, 'pb', 0, 0, axis_index_groups=x_groups, tiled=True)  2.43 us
  transfers between devices with their start and end apart: 9, of which 3 were waited for; matrix products, arithmetic and copies ran while one was open for 0% of the time, Pallas kernels for 3%

profile of v4, /device:TPU:1, one launch (start us, length us, event | category | flops | bytes accessed | tf_op | source)
XLA Modules:
  0.0 89.6 jit_solution(1608669711445284030)
XLA Ops:
  0.6 0.0 copy-start.4
  0.6 0.7 copy-done.4
  1.4 0.0 copy-start
  1.4 0.0 copy-start.1
  1.4 0.0 copy-start.2
  1.4 0.0 copy-start.3
  1.4 16.7 %all_to_all.15.near.refs_0_ = bf16[8,56,128]{2,1,0:T(8,128)(2,1)S(1)} all-to-all(bf16[8,56,128]{2,1,0:T(8,128)(2,1)S(1)} %spread.1), channel_id=1, replica_groups={{0,4,8,12,16,20,24,28},{1,5,9,13,17,21,25,29},{2,6,10,14,18,22,26,30},{..., dimensions={0} | all-to-all | bytes 229376 | tf_op jit(solution)/shard_map/all_to_all | solution.py:232
  18.1 2.7 %collective-permute-start.5 = (bf16[8,56,128]{2,1,0:T(8,128)(2,1)S(1)}, bf16[8,56,128]{2,1,0:T(8,128)(2,1)S(1)}, u32[]{:S(2)}, u32[]{:S(2)}) collective-permute-start(bf16[8,56,128]{2,1,0:T(8,128)(2,1)S(1)} %all_to_all.15.near.refs_0_), channel_id=1, source_target_pairs={{0,3},{1,0},{2,1},{3,2},{4,7},{5,4},{6,5},{7,6},{8,11},{9,8},{10,9... | collective-permute-start | bytes 344072 | tf_op jit(solution)/shard_map/ppermute | solution.py:236
  20.8 0.3 collective-permute-start.3
  21.2 0.7 collective-permute-start.1
  21.9 3.1 %collective-permute-start = (bf16[8,56,128]{2,1,0:T(8,128)(2,1)S(1)}, bf16[8,56,128]{2,1,0:T(8,128)(2,1)S(1)}, u32[]{:S(2)}, u32[]{:S(2)}) collective-permute-start(bf16[8,56,128]{2,1,0:T(8,128)(2,1)S(1)} %all_to_all.15.near.refs_0_), channel_id=1, source_target_pairs={{0,32},{32,0},{64,96},{96,64},{128,160},{160,128},{192,224},{224,1... | collective-permute-start | bytes 344072 | tf_op jit(solution)/shard_map/ppermute | solution.py:237
  25.0 0.0 collective-permute-done.5.refs_6_
  25.0 2.0 %collective-permute-start.6 = (bf16[8,56,128]{2,1,0:T(8,128)(2,1)S(1)}, bf16[8,56,128]{2,1,0:T(8,128)(2,1)S(1)}, u32[]{:S(2)}, u32[]{:S(2)}) collective-permute-start(bf16[8,56,128]{2,1,0:T(8,128)(2,1)S(1)} %collective-permute-done.5.refs_6_), channel_id=1, source_target_pairs={{0,32},{32,0},{64,96},{96,64},{128,160},{160,128},{192,224},{224,1... | collective-permute-start | bytes 344072 | tf_op jit(solution)/shard_map/ppermute | solution.py:237
  27.0 0.0 collective-permute-done.3.refs_4_
  27.0 2.8 %collective-permute-start.4 = (bf16[8,56,128]{2,1,0:T(8,128)(2,1)S(1)}, bf16[8,56,128]{2,1,0:T(8,128)(2,1)S(1)}, u32[]{:S(2)}, u32[]{:S(2)}) collective-permute-start(bf16[8,56,128]{2,1,0:T(8,128)(2,1)S(1)} %collective-permute-done.3.refs_4_), channel_id=1, source_target_pairs={{0,32},{32,0},{64,96},{96,64},{128,160},{160,128},{192,224},{224,1... | collective-permute-start | bytes 344072 | tf_op jit(solution)/shard_map/ppermute | solution.py:237
  29.8 0.0 collective-permute-done.1.refs_2_
  29.8 1.1 %collective-permute-start.2 = (bf16[8,56,128]{2,1,0:T(8,128)(2,1)S(1)}, bf16[8,56,128]{2,1,0:T(8,128)(2,1)S(1)}, u32[]{:S(2)}, u32[]{:S(2)}) collective-permute-start(bf16[8,56,128]{2,1,0:T(8,128)(2,1)S(1)} %collective-permute-done.1.refs_2_), channel_id=1, source_target_pairs={{0,32},{32,0},{64,96},{96,64},{128,160},{160,128},{192,224},{224,1... | collective-permute-start | bytes 344072 | tf_op jit(solution)/shard_map/ppermute | solution.py:237
  30.9 0.0 copy-done
  30.9 0.0 copy-done.1
  30.9 0.0 copy-done.2
  30.9 0.0 copy-done.3
  30.9 0.0 collective-permute-done.refs_1_
  30.9 0.0 collective-permute-done.6.refs_7_
  30.9 0.0 collective-permute-done.4.refs_5_
  30.9 0.9 %collective-permute-done.2.refs_3_ = bf16[8,56,128]{2,1,0:T(8,128)(2,1)S(1)} collective-permute-done((bf16[8,56,128]{2,1,0:T(8,128)(2,1)S(1)}, bf16[8,56,128]{2,1,0:T(8,128)(2,1)S(1)}, u32[]{:S(2)}, u32[]{:S(2)}) %collective-permute-start.2) | collective-permute-done | bytes 114720 | tf_op jit(solution)/shard_map/ppermute | solution.py:237
  31.9 3.8 %send_side.1 = (bf16[32,184,128]{2,1,0:T(8,128)(2,1)S(1)}, bf16[1792,256]{1,0:T(8,128)(2,1)S(1)}) custom-call(f32[8,128]{1,0:T(8,128)S(1)} %touch.1.token, bf16[2464,1792]{1,0:T(8,128)(2,1)S(1)} %bitcast.6, bf16[352,1792]{1,0:T(8,128)(2,1)S(1)} %bitcast.8, bf16[44,8,256]{2,1,0:T(8,128)(2,1)S(1)} %copy-done.3, bf16[44,56,256]{2,1,0:T(8,128)(2,1)S(1)} %bitcast.10, ...), custom_call_target="tpu_custom_call" | custom-call | tf_op jit(solution)/shard_map/send_side/pallas_call | solution.py:255
  35.7 39.0 %all_to_all.16.got = bf16[32,184,128]{2,1,0:T(8,128)(2,1)S(1)} all-to-all(bf16[32,184,128]{2,1,0:T(8,128)(2,1)S(1)} %get-tuple-element.7), channel_id=1, replica_groups={{0,4,8,12,16,20,24,28,1,5,9,13,17,21,25,29,2,6,10,14,18,22,26,30,3,7,11..., dimensions={0} | all-to-all | bytes 3014656 | tf_op jit(solution)/shard_map/all_to_all | solution.py:267
  74.7 1.1 %unpack.1 = (f32[8,1792]{1,0:T(8,128)S(1)}, bf16[1792,384]{1,0:T(8,128)(2,1)S(1)}, bf16[256,384]{1,0:T(8,128)(2,1)S(1)}) custom-call(bf16[32,184,128]{2,1,0:T(8,128)(2,1)S(1)} %all_to_all.16.got, bf16[1792,256]{1,0:T(8,128)(2,1)S(1)} %get-tuple-element.8.tt), custom_call_target="tpu_custom_call" | custom-call | tf_op jit(solution)/shard_map/unpack/pallas_call | solution.py:269
  75.8 2.9 %collective-permute-start.7 = (f32[8,1792]{1,0:T(8,128)S(1)}, f32[8,1792]{1,0:T(8,128)S(1)}, u32[]{:S(2)}, u32[]{:S(2)}) collective-permute-start(f32[8,1792]{1,0:T(8,128)S(1)} %get-tuple-element.11.own), channel_id=1, source_target_pairs={{0,32},{32,0},{64,96},{96,64},{128,160},{160,128},{192,224},{224,1... | collective-permute-start | bytes 172040 | tf_op jit(solution)/shard_map/ppermute | solution.py:290
  78.7 0.9 collective-permute-done.7.other
  79.6 0.7 both_cores.1
  80.3 4.0 %all-to-all-start.2 = ((bf16[4,8,1792]{2,1,0:T(8,128)(2,1)}), bf16[4,8,1792]{2,1,0:T(8,128)(2,1)S(1)}, u32[]{:S(2)}, u32[]{:S(2)}) async-start(bf16[4,8,1792]{2,1,0:T(8,128)(2,1)} %both_cores.1), calls=%async_computation.2 | async-start | bytes 229376 | tf_op jit(solution)/shard_map/all_to_all | solution.py:300
  84.2 2.3 %dress.1 = bf16[352,1792]{1,0:T(8,128)(2,1)} custom-call(bf16[1792,384]{1,0:T(8,128)(2,1)S(1)} %get-tuple-element.9.raw, bf16[256,384]{1,0:T(8,128)(2,1)S(1)} %get-tuple-element.10.lpt, bf16[1792,256]{1,0:T(8,128)(2,1)S(1)} %get-tuple-element.8.tt), custom_call_target="tpu_custom_call" | custom-call | flops 40000000000 | tf_op jit(solution)/shard_map/dress/pallas_call | solution.py:281
  86.6 2.4 %all-to-all-done.2 = bf16[4,8,1792]{2,1,0:T(8,128)(2,1)S(1)} async-done(((bf16[4,8,1792]{2,1,0:T(8,128)(2,1)}), bf16[4,8,1792]{2,1,0:T(8,128)(2,1)S(1)}, u32[]{:S(2)}, u32[]{:S(2)}) %all-to-all-start.2) | async-done | bytes 114720 | tf_op jit(solution)/shard_map/all_to_all | solution.py:300
  89.0 0.6 convert_reduce_fusion
  (2 shorter events, 0.0 us)
Async XLA Ops:
  0.6 0.7 copy-start.4
  1.4 29.5 %copy-start = (bf16[44,56,1792]{2,1,0:T(8,128)(2,1)S(1)}, bf16[44,56,1792]{2,1,0:T(8,128)(2,1)}, u32[]{:S(2)}) copy-start(bf16[44,56,1792]{2,1,0:T(8,128)(2,1)} %param.5) | copy-start | bytes 26492932
  1.4 29.5 %copy-start.1 = (bf16[44,8,1792]{2,1,0:T(8,128)(2,1)S(1)}, bf16[44,8,1792]{2,1,0:T(8,128)(2,1)}, u32[]{:S(2)}) copy-start(bf16[44,8,1792]{2,1,0:T(8,128)(2,1)} %param.6) | copy-start | bytes 3784708
  1.4 29.5 %copy-start.2 = (bf16[44,256,56]{1,2,0:T(8,128)(2,1)S(1)}, bf16[44,256,56]{1,2,0:T(8,128)(2,1)}, u32[]{:S(2)}) copy-start(bf16[44,256,56]{1,2,0:T(8,128)(2,1)} %param.8) | copy-start | bytes 3784708
  1.4 29.5 %copy-start.3 = (bf16[44,8,256]{2,1,0:T(8,128)(2,1)S(1)}, bf16[44,8,256]{2,1,0:T(8,128)(2,1)}, u32[]{:S(2)}) copy-start(bf16[44,8,256]{2,1,0:T(8,128)(2,1)} %oo.3) | copy-start | bytes 540676
  18.1 6.9 %collective-permute-start.5 = (bf16[8,56,128]{2,1,0:T(8,128)(2,1)S(1)}, bf16[8,56,128]{2,1,0:T(8,128)(2,1)S(1)}, u32[]{:S(2)}, u32[]{:S(2)}) collective-permute-start(bf16[8,56,128]{2,1,0:T(8,128)(2,1)S(1)} %all_to_all.15.near.refs_0_), channel_id=1, source_target_pairs={{0,3},{1,0},{2,1},{3,2},{4,7},{5,4},{6,5},{7,6},{8,11},{9,8},{10,9... | collective-permute-start | bytes 344072 | tf_op jit(solution)/shard_map/ppermute | solution.py:236
  20.8 6.2 %collective-permute-start.3 = (bf16[8,56,128]{2,1,0:T(8,128)(2,1)S(1)}, bf16[8,56,128]{2,1,0:T(8,128)(2,1)S(1)}, u32[]{:S(2)}, u32[]{:S(2)}) collective-permute-start(bf16[8,56,128]{2,1,0:T(8,128)(2,1)S(1)} %all_to_all.15.near.refs_0_), channel_id=1, source_target_pairs={{0,2},{1,3},{2,0},{3,1},{4,6},{5,7},{6,4},{7,5},{8,10},{9,11},{10,... | collective-permute-start | bytes 344072 | tf_op jit(solution)/shard_map/ppermute | solution.py:236
  21.2 8.6 %collective-permute-start.1 = (bf16[8,56,128]{2,1,0:T(8,128)(2,1)S(1)}, bf16[8,56,128]{2,1,0:T(8,128)(2,1)S(1)}, u32[]{:S(2)}, u32[]{:S(2)}) collective-permute-start(bf16[8,56,128]{2,1,0:T(8,128)(2,1)S(1)} %all_to_all.15.near.refs_0_), channel_id=1, source_target_pairs={{0,1},{1,2},{2,3},{3,0},{4,5},{5,6},{6,7},{7,4},{8,9},{9,10},{10,1... | collective-permute-start | bytes 344072 | tf_op jit(solution)/shard_map/ppermute | solution.py:236
  21.9 9.1 %collective-permute-start = (bf16[8,56,128]{2,1,0:T(8,128)(2,1)S(1)}, bf16[8,56,128]{2,1,0:T(8,128)(2,1)S(1)}, u32[]{:S(2)}, u32[]{:S(2)}) collective-permute-start(bf16[8,56,128]{2,1,0:T(8,128)(2,1)S(1)} %all_to_all.15.near.refs_0_), channel_id=1, source_target_pairs={{0,32},{32,0},{64,96},{96,64},{128,160},{160,128},{192,224},{224,1... | collective-permute-start | bytes 344072 | tf_op jit(solution)/shard_map/ppermute | solution.py:237
  25.0 6.0 %collective-permute-start.6 = (bf16[8,56,128]{2,1,0:T(8,128)(2,1)S(1)}, bf16[8,56,128]{2,1,0:T(8,128)(2,1)S(1)}, u32[]{:S(2)}, u32[]{:S(2)}) collective-permute-start(bf16[8,56,128]{2,1,0:T(8,128)(2,1)S(1)} %collective-permute-done.5.refs_6_), channel_id=1, source_target_pairs={{0,32},{32,0},{64,96},{96,64},{128,160},{160,128},{192,224},{224,1... | collective-permute-start | bytes 344072 | tf_op jit(solution)/shard_map/ppermute | solution.py:237
  27.0 4.0 %collective-permute-start.4 = (bf16[8,56,128]{2,1,0:T(8,128)(2,1)S(1)}, bf16[8,56,128]{2,1,0:T(8,128)(2,1)S(1)}, u32[]{:S(2)}, u32[]{:S(2)}) collective-permute-start(bf16[8,56,128]{2,1,0:T(8,128)(2,1)S(1)} %collective-permute-done.3.refs_4_), channel_id=1, source_target_pairs={{0,32},{32,0},{64,96},{96,64},{128,160},{160,128},{192,224},{224,1... | collective-permute-start | bytes 344072 | tf_op jit(solution)/shard_map/ppermute | solution.py:237
  29.8 2.1 %collective-permute-start.2 = (bf16[8,56,128]{2,1,0:T(8,128)(2,1)S(1)}, bf16[8,56,128]{2,1,0:T(8,128)(2,1)S(1)}, u32[]{:S(2)}, u32[]{:S(2)}) collective-permute-start(bf16[8,56,128]{2,1,0:T(8,128)(2,1)S(1)} %collective-permute-done.1.refs_2_), channel_id=1, source_target_pairs={{0,32},{32,0},{64,96},{96,64},{128,160},{160,128},{192,224},{224,1... | collective-permute-start | bytes 344072 | tf_op jit(solution)/shard_map/ppermute | solution.py:237
  75.8 3.8 %collective-permute-start.7 = (f32[8,1792]{1,0:T(8,128)S(1)}, f32[8,1792]{1,0:T(8,128)S(1)}, u32[]{:S(2)}, u32[]{:S(2)}) collective-permute-start(f32[8,1792]{1,0:T(8,128)S(1)} %get-tuple-element.11.own), channel_id=1, source_target_pairs={{0,32},{32,0},{64,96},{96,64},{128,160},{160,128},{192,224},{224,1... | collective-permute-start | bytes 172040 | tf_op jit(solution)/shard_map/ppermute | solution.py:290
  80.3 8.7 %all-to-all-start.2 = ((bf16[4,8,1792]{2,1,0:T(8,128)(2,1)}), bf16[4,8,1792]{2,1,0:T(8,128)(2,1)S(1)}, u32[]{:S(2)}, u32[]{:S(2)}) async-start(bf16[4,8,1792]{2,1,0:T(8,128)(2,1)} %both_cores.1), calls=%async_computation.2 | async-start | bytes 229376 | tf_op jit(solution)/shard_map/all_to_all | solution.py:300

commit v5 on v4

--- a/solution.py
+++ b/solution.py
@@ -16,12 +16,13 @@
 TN = (((0,), (0,)), ((), ()))
 
 
-ORDER = [z * NY + y for y in range(NY) for z in range(NZ)]
+Z_ORDER = list(reversed(range(NZ)))
+ORDER = [z * NY + y for y in range(NY) for z in reversed(range(NZ))]
 PLACE = [ORDER.index(p) for p in range(NZ * NY)]
 
 
 def z_groups():
-    return [[z * NY + y for z in range(NZ)] for y in range(NY)]
+    return [[z * NY + y for z in Z_ORDER] for y in range(NY)]
 
 
 def y_shift(k):
@@ -78,9 +79,9 @@
         src = (y - k + NY) & (NY - 1)
         for c in range(2):
             cols = pl.multiple_of((core if c == 0 else 1 - core) * LANES, LANES)
-            for z in range(NZ):
+            for k_z, z in enumerate(Z_ORDER):
                 at = pl.multiple_of((z * NY + src) * n_own, 8)
-                tt[pl.ds(at, n_own), pl.ds(cols, LANES)] = pieces[2 * k + c][z]
+                tt[pl.ds(at, n_own), pl.ds(cols, LANES)] = pieces[2 * k + c][k_z]
     amps = tt[...]
     lp = jnp.dot(ov[...], amps, preferred_element_type=F32).reshape(nq, OWN_I, nocc)
     d[:, n_own:, :] = (lp + oo[...].astype(F32)).astype(BF16).astype(F32)

time: 90.9 us -> 88.6 us (0.975)
  starting transfers between devices: 19.7 us -> 17.6 us
    all_to_all x1, blocking collectives: 39 us -> 41.8 us  [per_device(): lax.all_to_all(sent, 'pq', 0, 0, axis_index_groups=[ORDER], tiled=True)]
    all_to_all x1, blocking collectives: 16.7 us -> 14.1 us  [per_device(): lax.all_to_all(copies, 'pq', 0, 0, axis_index_groups=z_groups(), tiled=True)]
    ppermute x1, starting transfers between devices: 2.92 us -> 0.95 us  [per_device(): partner = lax.ppermute(fock, 'pb', other)]
where the time goes in v5:
time: 88.6 us; the launch traced here: 87.8 us
  blocking collectives  55.9 us (63%)
  starting transfers between devices  17.6 us (20%)
  Pallas kernels  7.9 us (9%)
  waiting for transfers between devices  4.24 us (5%)
    all_to_all x1, blocking collectives, per_device(): lax.all_to_all(sent, 'pq', 0, 0, axis_index_groups=[ORDER], tiled=True)  41.8 us
    all_to_all x1, blocking collectives, per_device(): lax.all_to_all(copies, 'pq', 0, 0, axis_index_groups=z_groups(), tiled=True)  14.1 us
    ppermute x4, starting transfers between devices, per_device(): lax.ppermute(piece, 'pb', other)  8.85 us
    all_to_all x1, starting transfers between devices, per_device(): lax.all_to_all(halves, 'pb', 0, 0, axis_index_groups=x_groups, tiled=True)  4.01 us
    pallas_call x1, Pallas kernels, per_device(): pl.pallas_call(send_side, out_shape=(jax.ShapeDtypeStruct((n_dev, sent_ro...  3.82 us
    ppermute x3, starting transfers between devices, per_device(): pieces.append(lax.ppermute(near, 'pq', y_shift(k)))  3.77 us
    all_to_all x1, waiting for transfers between devices, per_device(): lax.all_to_all(halves, 'pb', 0, 0, axis_index_groups=x_groups, tiled=True)  2.43 us
    pallas_call x1, Pallas kernels, per_device(): pl.pallas_call(dress, out_shape=jax.ShapeDtypeStruct((nq * OWN_I, nvirt),...  2.31 us
  transfers between devices with their start and end apart: 9, of which 3 were waited for; matrix products, arithmetic and copies ran while one was open for 0% of the time, Pallas kernels for 3%

profile of v5, /device:TPU:1, one launch (start us, length us, event | category | flops | bytes accessed | tf_op | source)
XLA Modules:
  0.0 87.8 jit_solution(10681974620805307409)
XLA Ops:
  0.6 0.0 copy-start.4
  0.6 0.7 copy-done.4
  1.4 0.0 copy-start
  1.4 0.0 copy-start.1
  1.4 0.0 copy-start.2
  1.4 0.0 copy-start.3
  1.4 14.1 %all_to_all.15.near.refs_0_ = bf16[8,56,128]{2,1,0:T(8,128)(2,1)S(1)} all-to-all(bf16[8,56,128]{2,1,0:T(8,128)(2,1)S(1)} %spread.1), channel_id=1, replica_groups={{28,24,20,16,12,8,4,0},{29,25,21,17,13,9,5,1},{30,26,22,18,14,10,6,2},{..., dimensions={0} | all-to-all | bytes 229376 | tf_op jit(solution)/shard_map/all_to_all | solution.py:233
  15.5 2.7 %collective-permute-start.5 = (bf16[8,56,128]{2,1,0:T(8,128)(2,1)S(1)}, bf16[8,56,128]{2,1,0:T(8,128)(2,1)S(1)}, u32[]{:S(2)}, u32[]{:S(2)}) collective-permute-start(bf16[8,56,128]{2,1,0:T(8,128)(2,1)S(1)} %all_to_all.15.near.refs_0_), channel_id=1, source_target_pairs={{0,3},{1,0},{2,1},{3,2},{4,7},{5,4},{6,5},{7,6},{8,11},{9,8},{10,9... | collective-permute-start | bytes 344072 | tf_op jit(solution)/shard_map/ppermute | solution.py:237
  18.3 0.3 collective-permute-start.3
  18.6 0.7 collective-permute-start.1
  19.3 2.9 %collective-permute-start = (bf16[8,56,128]{2,1,0:T(8,128)(2,1)S(1)}, bf16[8,56,128]{2,1,0:T(8,128)(2,1)S(1)}, u32[]{:S(2)}, u32[]{:S(2)}) collective-permute-start(bf16[8,56,128]{2,1,0:T(8,128)(2,1)S(1)} %all_to_all.15.near.refs_0_), channel_id=1, source_target_pairs={{0,32},{32,0},{64,96},{96,64},{128,160},{160,128},{192,224},{224,1... | collective-permute-start | bytes 344072 | tf_op jit(solution)/shard_map/ppermute | solution.py:238
  22.2 0.0 collective-permute-done.5.refs_6_
  22.2 2.2 %collective-permute-start.6 = (bf16[8,56,128]{2,1,0:T(8,128)(2,1)S(1)}, bf16[8,56,128]{2,1,0:T(8,128)(2,1)S(1)}, u32[]{:S(2)}, u32[]{:S(2)}) collective-permute-start(bf16[8,56,128]{2,1,0:T(8,128)(2,1)S(1)} %collective-permute-done.5.refs_6_), channel_id=1, source_target_pairs={{0,32},{32,0},{64,96},{96,64},{128,160},{160,128},{192,224},{224,1... | collective-permute-start | bytes 344072 | tf_op jit(solution)/shard_map/ppermute | solution.py:238
  24.4 0.0 collective-permute-done.3.refs_4_
  24.4 2.6 %collective-permute-start.4 = (bf16[8,56,128]{2,1,0:T(8,128)(2,1)S(1)}, bf16[8,56,128]{2,1,0:T(8,128)(2,1)S(1)}, u32[]{:S(2)}, u32[]{:S(2)}) collective-permute-start(bf16[8,56,128]{2,1,0:T(8,128)(2,1)S(1)} %collective-permute-done.3.refs_4_), channel_id=1, source_target_pairs={{0,32},{32,0},{64,96},{96,64},{128,160},{160,128},{192,224},{224,1... | collective-permute-start | bytes 344072 | tf_op jit(solution)/shard_map/ppermute | solution.py:238
  27.0 0.0 collective-permute-done.1.refs_2_
  27.0 1.1 %collective-permute-start.2 = (bf16[8,56,128]{2,1,0:T(8,128)(2,1)S(1)}, bf16[8,56,128]{2,1,0:T(8,128)(2,1)S(1)}, u32[]{:S(2)}, u32[]{:S(2)}) collective-permute-start(bf16[8,56,128]{2,1,0:T(8,128)(2,1)S(1)} %collective-permute-done.1.refs_2_), channel_id=1, source_target_pairs={{0,32},{32,0},{64,96},{96,64},{128,160},{160,128},{192,224},{224,1... | collective-permute-start | bytes 344072 | tf_op jit(solution)/shard_map/ppermute | solution.py:238
  28.2 0.0 copy-done
  28.2 0.0 copy-done.1
  28.2 0.0 copy-done.2
  28.2 0.0 copy-done.3
  28.2 0.0 collective-permute-done.refs_1_
  28.2 0.0 collective-permute-done.6.refs_7_
  28.2 0.0 collective-permute-done.4.refs_5_
  28.2 0.9 %collective-permute-done.2.refs_3_ = bf16[8,56,128]{2,1,0:T(8,128)(2,1)S(1)} collective-permute-done((bf16[8,56,128]{2,1,0:T(8,128)(2,1)S(1)}, bf16[8,56,128]{2,1,0:T(8,128)(2,1)S(1)}, u32[]{:S(2)}, u32[]{:S(2)}) %collective-permute-start.2) | collective-permute-done | bytes 114720 | tf_op jit(solution)/shard_map/ppermute | solution.py:238
  29.1 3.8 %send_side.1 = (bf16[32,184,128]{2,1,0:T(8,128)(2,1)S(1)}, bf16[1792,256]{1,0:T(8,128)(2,1)S(1)}) custom-call(f32[8,128]{1,0:T(8,128)S(1)} %touch.1.token, bf16[2464,1792]{1,0:T(8,128)(2,1)S(1)} %bitcast.6, bf16[352,1792]{1,0:T(8,128)(2,1)S(1)} %bitcast.8, bf16[44,8,256]{2,1,0:T(8,128)(2,1)S(1)} %copy-done.3, bf16[44,56,256]{2,1,0:T(8,128)(2,1)S(1)} %bitcast.10, ...), custom_call_target="tpu_custom_call" | custom-call | tf_op jit(solution)/shard_map/send_side/pallas_call | solution.py:256
  33.0 41.8 %all_to_all.16.got = bf16[32,184,128]{2,1,0:T(8,128)(2,1)S(1)} all-to-all(bf16[32,184,128]{2,1,0:T(8,128)(2,1)S(1)} %get-tuple-element.7), channel_id=1, replica_groups={{28,24,20,16,12,8,4,0,29,25,21,17,13,9,5,1,30,26,22,18,14,10,6,2,31,27,..., dimensions={0} | all-to-all | bytes 3014656 | tf_op jit(solution)/shard_map/all_to_all | solution.py:268
  74.8 1.1 %unpack.1 = (f32[8,1792]{1,0:T(8,128)S(1)}, bf16[1792,384]{1,0:T(8,128)(2,1)S(1)}, bf16[256,384]{1,0:T(8,128)(2,1)S(1)}) custom-call(bf16[32,184,128]{2,1,0:T(8,128)(2,1)S(1)} %all_to_all.16.got, bf16[1792,256]{1,0:T(8,128)(2,1)S(1)} %get-tuple-element.8.tt), custom_call_target="tpu_custom_call" | custom-call | tf_op jit(solution)/shard_map/unpack/pallas_call | solution.py:270
  75.9 0.9 %collective-permute-start.7 = (f32[8,1792]{1,0:T(8,128)S(1)}, f32[8,1792]{1,0:T(8,128)S(1)}, u32[]{:S(2)}, u32[]{:S(2)}) collective-permute-start(f32[8,1792]{1,0:T(8,128)S(1)} %get-tuple-element.11.own), channel_id=1, source_target_pairs={{0,32},{32,0},{64,96},{96,64},{128,160},{160,128},{192,224},{224,1... | collective-permute-start | bytes 172040 | tf_op jit(solution)/shard_map/ppermute | solution.py:291
  76.8 0.9 %collective-permute-done.7.other = f32[8,1792]{1,0:T(8,128)S(1)} collective-permute-done((f32[8,1792]{1,0:T(8,128)S(1)}, f32[8,1792]{1,0:T(8,128)S(1)}, u32[]{:S(2)}, u32[]{:S(2)}) %collective-permute-start.7) | collective-permute-done | bytes 57376 | tf_op jit(solution)/shard_map/ppermute | solution.py:291
  77.7 0.7 both_cores.1
  78.4 4.0 %all-to-all-start.2 = ((bf16[4,8,1792]{2,1,0:T(8,128)(2,1)}), bf16[4,8,1792]{2,1,0:T(8,128)(2,1)S(1)}, u32[]{:S(2)}, u32[]{:S(2)}) async-start(bf16[4,8,1792]{2,1,0:T(8,128)(2,1)} %both_cores.1), calls=%async_computation.2 | async-start | bytes 229376 | tf_op jit(solution)/shard_map/all_to_all | solution.py:301
  82.4 2.3 %dress.1 = bf16[352,1792]{1,0:T(8,128)(2,1)} custom-call(bf16[1792,384]{1,0:T(8,128)(2,1)S(1)} %get-tuple-element.9.raw, bf16[256,384]{1,0:T(8,128)(2,1)S(1)} %get-tuple-element.10.lpt, bf16[1792,256]{1,0:T(8,128)(2,1)S(1)} %get-tuple-element.8.tt), custom_call_target="tpu_custom_call" | custom-call | flops 40000000000 | tf_op jit(solution)/shard_map/dress/pallas_call | solution.py:282
  84.7 2.4 %all-to-all-done.2 = bf16[4,8,1792]{2,1,0:T(8,128)(2,1)S(1)} async-done(((bf16[4,8,1792]{2,1,0:T(8,128)(2,1)}), bf16[4,8,1792]{2,1,0:T(8,128)(2,1)S(1)}, u32[]{:S(2)}, u32[]{:S(2)}) %all-to-all-start.2) | async-done | bytes 114720 | tf_op jit(solution)/shard_map/all_to_all | solution.py:301
  87.1 0.6 convert_reduce_fusion
  (2 shorter events, 0.0 us)
Async XLA Ops:
  0.6 0.7 copy-start.4
  1.4 26.8 %copy-start = (bf16[44,56,1792]{2,1,0:T(8,128)(2,1)S(1)}, bf16[44,56,1792]{2,1,0:T(8,128)(2,1)}, u32[]{:S(2)}) copy-start(bf16[44,56,1792]{2,1,0:T(8,128)(2,1)} %param.5) | copy-start | bytes 26492932
  1.4 26.8 %copy-start.1 = (bf16[44,8,1792]{2,1,0:T(8,128)(2,1)S(1)}, bf16[44,8,1792]{2,1,0:T(8,128)(2,1)}, u32[]{:S(2)}) copy-start(bf16[44,8,1792]{2,1,0:T(8,128)(2,1)} %param.6) | copy-start | bytes 3784708
  1.4 26.8 %copy-start.2 = (bf16[44,256,56]{1,2,0:T(8,128)(2,1)S(1)}, bf16[44,256,56]{1,2,0:T(8,128)(2,1)}, u32[]{:S(2)}) copy-start(bf16[44,256,56]{1,2,0:T(8,128)(2,1)} %param.8) | copy-start | bytes 3784708
  1.4 26.8 %copy-start.3 = (bf16[44,8,256]{2,1,0:T(8,128)(2,1)S(1)}, bf16[44,8,256]{2,1,0:T(8,128)(2,1)}, u32[]{:S(2)}) copy-start(bf16[44,8,256]{2,1,0:T(8,128)(2,1)} %oo.3) | copy-start | bytes 540676
  15.5 6.7 %collective-permute-start.5 = (bf16[8,56,128]{2,1,0:T(8,128)(2,1)S(1)}, bf16[8,56,128]{2,1,0:T(8,128)(2,1)S(1)}, u32[]{:S(2)}, u32[]{:S(2)}) collective-permute-start(bf16[8,56,128]{2,1,0:T(8,128)(2,1)S(1)} %all_to_all.15.near.refs_0_), channel_id=1, source_target_pairs={{0,3},{1,0},{2,1},{3,2},{4,7},{5,4},{6,5},{7,6},{8,11},{9,8},{10,9... | collective-permute-start | bytes 344072 | tf_op jit(solution)/shard_map/ppermute | solution.py:237
  18.3 6.2 %collective-permute-start.3 = (bf16[8,56,128]{2,1,0:T(8,128)(2,1)S(1)}, bf16[8,56,128]{2,1,0:T(8,128)(2,1)S(1)}, u32[]{:S(2)}, u32[]{:S(2)}) collective-permute-start(bf16[8,56,128]{2,1,0:T(8,128)(2,1)S(1)} %all_to_all.15.near.refs_0_), channel_id=1, source_target_pairs={{0,2},{1,3},{2,0},{3,1},{4,6},{5,7},{6,4},{7,5},{8,10},{9,11},{10,... | collective-permute-start | bytes 344072 | tf_op jit(solution)/shard_map/ppermute | solution.py:237
  18.6 8.4 %collective-permute-start.1 = (bf16[8,56,128]{2,1,0:T(8,128)(2,1)S(1)}, bf16[8,56,128]{2,1,0:T(8,128)(2,1)S(1)}, u32[]{:S(2)}, u32[]{:S(2)}) collective-permute-start(bf16[8,56,128]{2,1,0:T(8,128)(2,1)S(1)} %all_to_all.15.near.refs_0_), channel_id=1, source_target_pairs={{0,1},{1,2},{2,3},{3,0},{4,5},{5,6},{6,7},{7,4},{8,9},{9,10},{10,1... | collective-permute-start | bytes 344072 | tf_op jit(solution)/shard_map/ppermute | solution.py:237
  19.3 8.9 %collective-permute-start = (bf16[8,56,128]{2,1,0:T(8,128)(2,1)S(1)}, bf16[8,56,128]{2,1,0:T(8,128)(2,1)S(1)}, u32[]{:S(2)}, u32[]{:S(2)}) collective-permute-start(bf16[8,56,128]{2,1,0:T(8,128)(2,1)S(1)} %all_to_all.15.near.refs_0_), channel_id=1, source_target_pairs={{0,32},{32,0},{64,96},{96,64},{128,160},{160,128},{192,224},{224,1... | collective-permute-start | bytes 344072 | tf_op jit(solution)/shard_map/ppermute | solution.py:238
  22.2 6.0 %collective-permute-start.6 = (bf16[8,56,128]{2,1,0:T(8,128)(2,1)S(1)}, bf16[8,56,128]{2,1,0:T(8,128)(2,1)S(1)}, u32[]{:S(2)}, u32[]{:S(2)}) collective-permute-start(bf16[8,56,128]{2,1,0:T(8,128)(2,1)S(1)} %collective-permute-done.5.refs_6_), channel_id=1, source_target_pairs={{0,32},{32,0},{64,96},{96,64},{128,160},{160,128},{192,224},{224,1... | collective-permute-start | bytes 344072 | tf_op jit(solution)/shard_map/ppermute | solution.py:238
  24.4 3.8 %collective-permute-start.4 = (bf16[8,56,128]{2,1,0:T(8,128)(2,1)S(1)}, bf16[8,56,128]{2,1,0:T(8,128)(2,1)S(1)}, u32[]{:S(2)}, u32[]{:S(2)}) collective-permute-start(bf16[8,56,128]{2,1,0:T(8,128)(2,1)S(1)} %collective-permute-done.3.refs_4_), channel_id=1, source_target_pairs={{0,32},{32,0},{64,96},{96,64},{128,160},{160,128},{192,224},{224,1... | collective-permute-start | bytes 344072 | tf_op jit(solution)/shard_map/ppermute | solution.py:238
  27.0 2.1 %collective-permute-start.2 = (bf16[8,56,128]{2,1,0:T(8,128)(2,1)S(1)}, bf16[8,56,128]{2,1,0:T(8,128)(2,1)S(1)}, u32[]{:S(2)}, u32[]{:S(2)}) collective-permute-start(bf16[8,56,128]{2,1,0:T(8,128)(2,1)S(1)} %collective-permute-done.1.refs_2_), channel_id=1, source_target_pairs={{0,32},{32,0},{64,96},{96,64},{128,160},{160,128},{192,224},{224,1... | collective-permute-start | bytes 344072 | tf_op jit(solution)/shard_map/ppermute | solution.py:238
  75.9 1.8 %collective-permute-start.7 = (f32[8,1792]{1,0:T(8,128)S(1)}, f32[8,1792]{1,0:T(8,128)S(1)}, u32[]{:S(2)}, u32[]{:S(2)}) collective-permute-start(f32[8,1792]{1,0:T(8,128)S(1)} %get-tuple-element.11.own), channel_id=1, source_target_pairs={{0,32},{32,0},{64,96},{96,64},{128,160},{160,128},{192,224},{224,1... | collective-permute-start | bytes 172040 | tf_op jit(solution)/shard_map/ppermute | solution.py:291
  78.4 8.8 %all-to-all-start.2 = ((bf16[4,8,1792]{2,1,0:T(8,128)(2,1)}), bf16[4,8,1792]{2,1,0:T(8,128)(2,1)S(1)}, u32[]{:S(2)}, u32[]{:S(2)}) async-start(bf16[4,8,1792]{2,1,0:T(8,128)(2,1)} %both_cores.1), calls=%async_computation.2 | async-start | bytes 229376 | tf_op jit(solution)/shard_map/all_to_all | solution.py:301

commit v6 on v5

--- a/solution.py
+++ b/solution.py
@@ -17,7 +17,7 @@
 
 
 Z_ORDER = list(reversed(range(NZ)))
-ORDER = [z * NY + y for y in range(NY) for z in reversed(range(NZ))]
+ORDER = [z * NY + y for z in reversed(range(NZ)) for y in range(NY)]
 PLACE = [ORDER.index(p) for p in range(NZ * NY)]
 
 
@@ -76,7 +76,7 @@
     core = lax.axis_index("pb") & 1
     y = me & (NY - 1)
     for k in range(NY):
-        src = (y - k + NY) & (NY - 1)
+        src = (y + k) & (NY - 1)
         for c in range(2):
             cols = pl.multiple_of((core if c == 0 else 1 - core) * LANES, LANES)
             for k_z, z in enumerate(Z_ORDER):
@@ -234,7 +234,7 @@
     other = [(b, b ^ 1) for b in range(n_pb)]
     pieces = [near]
     for k in range(1, NY):
-        pieces.append(lax.ppermute(near, "pq", y_shift(k)))
+        pieces.append(lax.ppermute(near, "pq", y_shift(NY - k)))
     pieces = [p for piece in pieces for p in (piece, lax.ppermute(piece, "pb", other))]
     blocks = (
         chol_vv.reshape(nq * n_own, nvirt),
@@ -297,7 +297,7 @@
         compiler_params=PARAMS,
         name="both_cores",
     )(fock, partner)
-    x_groups = [list(range(c, n_pb, 2)) for c in range(2)]
+    x_groups = [list(range(c, n_pb, 2))[::-1] for c in range(2)]
     parts = lax.all_to_all(halves, "pb", 0, 0, axis_index_groups=x_groups, tiled=True)
     fock_ov = jnp.sum(parts.astype(F32), axis=0)
     return dressed.reshape(nq, OWN_I, nvirt), fock_ov

time: 88.6 us -> 87.9 us (level)
  starting transfers between devices: 17.6 us -> 19.7 us
  waiting for transfers between devices: 4.24 us -> 2.46 us
    ppermute x4, starting transfers between devices: 8.85 us -> 6.37 us  [per_device(): lax.ppermute(piece, 'pb', other)]
    all_to_all x1, waiting for transfers between devices: 2.43 us -> 0.64 us  [per_device(): lax.all_to_all(halves, 'pb', 0, 0, axis_index_groups=x_groups, tiled=True)]
    all_to_all x1, starting transfers between devices: 4.01 us -> 5.75 us  [per_device(): lax.all_to_all(halves, 'pb', 0, 0, axis_index_groups=x_groups, tiled=True)]
    ppermute x1, starting transfers between devices: 0.95 us -> 2.6 us  [per_device(): partner = lax.ppermute(fock, 'pb', other)]
    ppermute x3, starting transfers between devices: 3.77 us -> 4.99 us  [per_device(): pieces.append(lax.ppermute(near, 'pq', y_shift(NY - k)))]
  transfers between devices with their start and end apart: 9 -> 9, of which waited for: 3 -> 4; matrix products, arithmetic and copies ran while one was open for 0% -> 0% of each run, Pallas kernels for 3% -> 3%
where the time goes in v6:
time: 87.9 us; the launch traced here: 87.6 us
  blocking collectives  55.5 us (63%)
  starting transfers between devices  19.7 us (22%)
  Pallas kernels  7.89 us (9%)
  waiting for transfers between devices  2.46 us (3%)
    all_to_all x1, blocking collectives, per_device(): lax.all_to_all(sent, 'pq', 0, 0, axis_index_groups=[ORDER], tiled=True)  41.4 us
    all_to_all x1, blocking collectives, per_device(): lax.all_to_all(copies, 'pq', 0, 0, axis_index_groups=z_groups(), tiled=True)  14.1 us
    ppermute x4, starting transfers between devices, per_device(): lax.ppermute(piece, 'pb', other)  6.37 us
    all_to_all x1, starting transfers between devices, per_device(): lax.all_to_all(halves, 'pb', 0, 0, axis_index_groups=x_groups, tiled=True)  5.75 us
    ppermute x3, starting transfers between devices, per_device(): pieces.append(lax.ppermute(near, 'pq', y_shift(NY - k)))  4.99 us
    pallas_call x1, Pallas kernels, per_device(): pl.pallas_call(send_side, out_shape=(jax.ShapeDtypeStruct((n_dev, sent_ro...  3.82 us
    ppermute x1, starting transfers between devices, per_device(): partner = lax.ppermute(fock, 'pb', other)  2.6 us
    pallas_call x1, Pallas kernels, per_device(): pl.pallas_call(dress, out_shape=jax.ShapeDtypeStruct((nq * OWN_I, nvirt),...  2.31 us
  transfers between devices with their start and end apart: 9, of which 4 were waited for; matrix products, arithmetic and copies ran while one was open for 0% of the time, Pallas kernels for 3%

profile of v6, /device:TPU:1, one launch (start us, length us, event | category | flops | bytes accessed | tf_op | source)
XLA Modules:
  0.0 87.6 jit_solution(14441438376987616567)
XLA Ops:
  0.6 0.0 copy-start.4
  0.6 0.7 copy-done.4
  1.4 0.0 copy-start
  1.4 0.0 copy-start.1
  1.4 0.0 copy-start.2
  1.4 0.0 copy-start.3
  1.4 14.1 %all_to_all.15.near.refs_0_ = bf16[8,56,128]{2,1,0:T(8,128)(2,1)S(1)} all-to-all(bf16[8,56,128]{2,1,0:T(8,128)(2,1)S(1)} %spread.1), channel_id=1, replica_groups={{28,24,20,16,12,8,4,0},{29,25,21,17,13,9,5,1},{30,26,22,18,14,10,6,2},{..., dimensions={0} | all-to-all | bytes 229376 | tf_op jit(solution)/shard_map/all_to_all | solution.py:233
  15.5 1.3 %collective-permute-start.5 = (bf16[8,56,128]{2,1,0:T(8,128)(2,1)S(1)}, bf16[8,56,128]{2,1,0:T(8,128)(2,1)S(1)}, u32[]{:S(2)}, u32[]{:S(2)}) collective-permute-start(bf16[8,56,128]{2,1,0:T(8,128)(2,1)S(1)} %all_to_all.15.near.refs_0_), channel_id=1, source_target_pairs={{0,1},{1,2},{2,3},{3,0},{4,5},{5,6},{6,7},{7,4},{8,9},{9,10},{10,1... | collective-permute-start | bytes 344072 | tf_op jit(solution)/shard_map/ppermute | solution.py:237
  16.8 2.6 %collective-permute-start.3 = (bf16[8,56,128]{2,1,0:T(8,128)(2,1)S(1)}, bf16[8,56,128]{2,1,0:T(8,128)(2,1)S(1)}, u32[]{:S(2)}, u32[]{:S(2)}) collective-permute-start(bf16[8,56,128]{2,1,0:T(8,128)(2,1)S(1)} %all_to_all.15.near.refs_0_), channel_id=1, source_target_pairs={{0,2},{1,3},{2,0},{3,1},{4,6},{5,7},{6,4},{7,5},{8,10},{9,11},{10,... | collective-permute-start | bytes 344072 | tf_op jit(solution)/shard_map/ppermute | solution.py:237
  19.4 1.1 %collective-permute-start.1 = (bf16[8,56,128]{2,1,0:T(8,128)(2,1)S(1)}, bf16[8,56,128]{2,1,0:T(8,128)(2,1)S(1)}, u32[]{:S(2)}, u32[]{:S(2)}) collective-permute-start(bf16[8,56,128]{2,1,0:T(8,128)(2,1)S(1)} %all_to_all.15.near.refs_0_), channel_id=1, source_target_pairs={{0,3},{1,0},{2,1},{3,2},{4,7},{5,4},{6,5},{7,6},{8,11},{9,8},{10,9... | collective-permute-start | bytes 344072 | tf_op jit(solution)/shard_map/ppermute | solution.py:237
  20.5 2.9 %collective-permute-start = (bf16[8,56,128]{2,1,0:T(8,128)(2,1)S(1)}, bf16[8,56,128]{2,1,0:T(8,128)(2,1)S(1)}, u32[]{:S(2)}, u32[]{:S(2)}) collective-permute-start(bf16[8,56,128]{2,1,0:T(8,128)(2,1)S(1)} %all_to_all.15.near.refs_0_), channel_id=1, source_target_pairs={{0,32},{32,0},{64,96},{96,64},{128,160},{160,128},{192,224},{224,1... | collective-permute-start | bytes 344072 | tf_op jit(solution)/shard_map/ppermute | solution.py:238
  23.5 0.0 collective-permute-done.5.refs_6_
  23.5 1.3 %collective-permute-start.6 = (bf16[8,56,128]{2,1,0:T(8,128)(2,1)S(1)}, bf16[8,56,128]{2,1,0:T(8,128)(2,1)S(1)}, u32[]{:S(2)}, u32[]{:S(2)}) collective-permute-start(bf16[8,56,128]{2,1,0:T(8,128)(2,1)S(1)} %collective-permute-done.5.refs_6_), channel_id=1, source_target_pairs={{0,32},{32,0},{64,96},{96,64},{128,160},{160,128},{192,224},{224,1... | collective-permute-start | bytes 344072 | tf_op jit(solution)/shard_map/ppermute | solution.py:238
  24.8 0.0 collective-permute-done.3.refs_4_
  24.8 1.3 %collective-permute-start.4 = (bf16[8,56,128]{2,1,0:T(8,128)(2,1)S(1)}, bf16[8,56,128]{2,1,0:T(8,128)(2,1)S(1)}, u32[]{:S(2)}, u32[]{:S(2)}) collective-permute-start(bf16[8,56,128]{2,1,0:T(8,128)(2,1)S(1)} %collective-permute-done.3.refs_4_), channel_id=1, source_target_pairs={{0,32},{32,0},{64,96},{96,64},{128,160},{160,128},{192,224},{224,1... | collective-permute-start | bytes 344072 | tf_op jit(solution)/shard_map/ppermute | solution.py:238
  26.1 0.0 collective-permute-done.1.refs_2_
  26.1 0.8 collective-permute-start.2
  26.9 0.0 copy-done
  26.9 0.0 copy-done.1
  26.9 0.0 copy-done.2
  26.9 0.0 copy-done.3
  26.9 0.0 collective-permute-done.refs_1_
  26.9 0.0 collective-permute-done.6.refs_7_
  26.9 0.1 collective-permute-done.4.refs_5_
  27.1 0.8 collective-permute-done.2.refs_3_
  27.9 3.8 %send_side.1 = (bf16[32,184,128]{2,1,0:T(8,128)(2,1)S(1)}, bf16[1792,256]{1,0:T(8,128)(2,1)S(1)}) custom-call(f32[8,128]{1,0:T(8,128)S(1)} %touch.1.token, bf16[2464,1792]{1,0:T(8,128)(2,1)S(1)} %bitcast.6, bf16[352,1792]{1,0:T(8,128)(2,1)S(1)} %bitcast.8, bf16[44,8,256]{2,1,0:T(8,128)(2,1)S(1)} %copy-done.3, bf16[44,56,256]{2,1,0:T(8,128)(2,1)S(1)} %bitcast.10, ...), custom_call_target="tpu_custom_call" | custom-call | tf_op jit(solution)/shard_map/send_side/pallas_call | solution.py:256
  31.7 41.4 %all_to_all.16.got = bf16[32,184,128]{2,1,0:T(8,128)(2,1)S(1)} all-to-all(bf16[32,184,128]{2,1,0:T(8,128)(2,1)S(1)} %get-tuple-element.7), channel_id=1, replica_groups={{28,29,30,31,24,25,26,27,20,21,22,23,16,17,18,19,12,13,14,15,8,9,10,11,..., dimensions={0} | all-to-all | bytes 3014656 | tf_op jit(solution)/shard_map/all_to_all | solution.py:268
  73.1 1.1 %unpack.1 = (f32[8,1792]{1,0:T(8,128)S(1)}, bf16[1792,384]{1,0:T(8,128)(2,1)S(1)}, bf16[256,384]{1,0:T(8,128)(2,1)S(1)}) custom-call(bf16[32,184,128]{2,1,0:T(8,128)(2,1)S(1)} %all_to_all.16.got, bf16[1792,256]{1,0:T(8,128)(2,1)S(1)} %get-tuple-element.8.tt), custom_call_target="tpu_custom_call" | custom-call | tf_op jit(solution)/shard_map/unpack/pallas_call | solution.py:270
  74.1 2.6 %collective-permute-start.7 = (f32[8,1792]{1,0:T(8,128)S(1)}, f32[8,1792]{1,0:T(8,128)S(1)}, u32[]{:S(2)}, u32[]{:S(2)}) collective-permute-start(f32[8,1792]{1,0:T(8,128)S(1)} %get-tuple-element.11.own), channel_id=1, source_target_pairs={{0,32},{32,0},{64,96},{96,64},{128,160},{160,128},{192,224},{224,1... | collective-permute-start | bytes 172040 | tf_op jit(solution)/shard_map/ppermute | solution.py:291
  76.7 0.9 %collective-permute-done.7.other = f32[8,1792]{1,0:T(8,128)S(1)} collective-permute-done((f32[8,1792]{1,0:T(8,128)S(1)}, f32[8,1792]{1,0:T(8,128)S(1)}, u32[]{:S(2)}, u32[]{:S(2)}) %collective-permute-start.7) | collective-permute-done | bytes 57376 | tf_op jit(solution)/shard_map/ppermute | solution.py:291
  77.6 0.7 both_cores.1
  78.3 5.7 %all-to-all-start.2 = ((bf16[4,8,1792]{2,1,0:T(8,128)(2,1)}), bf16[4,8,1792]{2,1,0:T(8,128)(2,1)S(1)}, u32[]{:S(2)}, u32[]{:S(2)}) async-start(bf16[4,8,1792]{2,1,0:T(8,128)(2,1)} %both_cores.1), calls=%async_computation.2 | async-start | bytes 229376 | tf_op jit(solution)/shard_map/all_to_all | solution.py:301
  84.0 2.3 %dress.1 = bf16[352,1792]{1,0:T(8,128)(2,1)} custom-call(bf16[1792,384]{1,0:T(8,128)(2,1)S(1)} %get-tuple-element.9.raw, bf16[256,384]{1,0:T(8,128)(2,1)S(1)} %get-tuple-element.10.lpt, bf16[1792,256]{1,0:T(8,128)(2,1)S(1)} %get-tuple-element.8.tt), custom_call_target="tpu_custom_call" | custom-call | flops 40000000000 | tf_op jit(solution)/shard_map/dress/pallas_call | solution.py:282
  86.4 0.6 all-to-all-done.2
  87.0 0.6 convert_reduce_fusion
  (2 shorter events, 0.0 us)
Async XLA Ops:
  0.6 0.7 copy-start.4
  1.4 25.5 %copy-start = (bf16[44,56,1792]{2,1,0:T(8,128)(2,1)S(1)}, bf16[44,56,1792]{2,1,0:T(8,128)(2,1)}, u32[]{:S(2)}) copy-start(bf16[44,56,1792]{2,1,0:T(8,128)(2,1)} %param.5) | copy-start | bytes 26492932
  1.4 25.5 %copy-start.1 = (bf16[44,8,1792]{2,1,0:T(8,128)(2,1)S(1)}, bf16[44,8,1792]{2,1,0:T(8,128)(2,1)}, u32[]{:S(2)}) copy-start(bf16[44,8,1792]{2,1,0:T(8,128)(2,1)} %param.6) | copy-start | bytes 3784708
  1.4 25.5 %copy-start.2 = (bf16[44,256,56]{1,2,0:T(8,128)(2,1)S(1)}, bf16[44,256,56]{1,2,0:T(8,128)(2,1)}, u32[]{:S(2)}) copy-start(bf16[44,256,56]{1,2,0:T(8,128)(2,1)} %param.8) | copy-start | bytes 3784708
  1.4 25.5 %copy-start.3 = (bf16[44,8,256]{2,1,0:T(8,128)(2,1)S(1)}, bf16[44,8,256]{2,1,0:T(8,128)(2,1)}, u32[]{:S(2)}) copy-start(bf16[44,8,256]{2,1,0:T(8,128)(2,1)} %oo.3) | copy-start | bytes 540676
  15.5 7.9 %collective-permute-start.5 = (bf16[8,56,128]{2,1,0:T(8,128)(2,1)S(1)}, bf16[8,56,128]{2,1,0:T(8,128)(2,1)S(1)}, u32[]{:S(2)}, u32[]{:S(2)}) collective-permute-start(bf16[8,56,128]{2,1,0:T(8,128)(2,1)S(1)} %all_to_all.15.near.refs_0_), channel_id=1, source_target_pairs={{0,1},{1,2},{2,3},{3,0},{4,5},{5,6},{6,7},{7,4},{8,9},{9,10},{10,1... | collective-permute-start | bytes 344072 | tf_op jit(solution)/shard_map/ppermute | solution.py:237
  16.8 7.9 %collective-permute-start.3 = (bf16[8,56,128]{2,1,0:T(8,128)(2,1)S(1)}, bf16[8,56,128]{2,1,0:T(8,128)(2,1)S(1)}, u32[]{:S(2)}, u32[]{:S(2)}) collective-permute-start(bf16[8,56,128]{2,1,0:T(8,128)(2,1)S(1)} %all_to_all.15.near.refs_0_), channel_id=1, source_target_pairs={{0,2},{1,3},{2,0},{3,1},{4,6},{5,7},{6,4},{7,5},{8,10},{9,11},{10,... | collective-permute-start | bytes 344072 | tf_op jit(solution)/shard_map/ppermute | solution.py:237
  19.4 6.7 %collective-permute-start.1 = (bf16[8,56,128]{2,1,0:T(8,128)(2,1)S(1)}, bf16[8,56,128]{2,1,0:T(8,128)(2,1)S(1)}, u32[]{:S(2)}, u32[]{:S(2)}) collective-permute-start(bf16[8,56,128]{2,1,0:T(8,128)(2,1)S(1)} %all_to_all.15.near.refs_0_), channel_id=1, source_target_pairs={{0,3},{1,0},{2,1},{3,2},{4,7},{5,4},{6,5},{7,6},{8,11},{9,8},{10,9... | collective-permute-start | bytes 344072 | tf_op jit(solution)/shard_map/ppermute | solution.py:237
  20.5 6.4 %collective-permute-start = (bf16[8,56,128]{2,1,0:T(8,128)(2,1)S(1)}, bf16[8,56,128]{2,1,0:T(8,128)(2,1)S(1)}, u32[]{:S(2)}, u32[]{:S(2)}) collective-permute-start(bf16[8,56,128]{2,1,0:T(8,128)(2,1)S(1)} %all_to_all.15.near.refs_0_), channel_id=1, source_target_pairs={{0,32},{32,0},{64,96},{96,64},{128,160},{160,128},{192,224},{224,1... | collective-permute-start | bytes 344072 | tf_op jit(solution)/shard_map/ppermute | solution.py:238
  23.5 3.5 %collective-permute-start.6 = (bf16[8,56,128]{2,1,0:T(8,128)(2,1)S(1)}, bf16[8,56,128]{2,1,0:T(8,128)(2,1)S(1)}, u32[]{:S(2)}, u32[]{:S(2)}) collective-permute-start(bf16[8,56,128]{2,1,0:T(8,128)(2,1)S(1)} %collective-permute-done.5.refs_6_), channel_id=1, source_target_pairs={{0,32},{32,0},{64,96},{96,64},{128,160},{160,128},{192,224},{224,1... | collective-permute-start | bytes 344072 | tf_op jit(solution)/shard_map/ppermute | solution.py:238
  24.8 2.3 %collective-permute-start.4 = (bf16[8,56,128]{2,1,0:T(8,128)(2,1)S(1)}, bf16[8,56,128]{2,1,0:T(8,128)(2,1)S(1)}, u32[]{:S(2)}, u32[]{:S(2)}) collective-permute-start(bf16[8,56,128]{2,1,0:T(8,128)(2,1)S(1)} %collective-permute-done.3.refs_4_), channel_id=1, source_target_pairs={{0,32},{32,0},{64,96},{96,64},{128,160},{160,128},{192,224},{224,1... | collective-permute-start | bytes 344072 | tf_op jit(solution)/shard_map/ppermute | solution.py:238
  26.1 1.8 %collective-permute-start.2 = (bf16[8,56,128]{2,1,0:T(8,128)(2,1)S(1)}, bf16[8,56,128]{2,1,0:T(8,128)(2,1)S(1)}, u32[]{:S(2)}, u32[]{:S(2)}) collective-permute-start(bf16[8,56,128]{2,1,0:T(8,128)(2,1)S(1)} %collective-permute-done.1.refs_2_), channel_id=1, source_target_pairs={{0,32},{32,0},{64,96},{96,64},{128,160},{160,128},{192,224},{224,1... | collective-permute-start | bytes 344072 | tf_op jit(solution)/shard_map/ppermute | solution.py:238
  74.1 3.5 %collective-permute-start.7 = (f32[8,1792]{1,0:T(8,128)S(1)}, f32[8,1792]{1,0:T(8,128)S(1)}, u32[]{:S(2)}, u32[]{:S(2)}) collective-permute-start(f32[8,1792]{1,0:T(8,128)S(1)} %get-tuple-element.11.own), channel_id=1, source_target_pairs={{0,32},{32,0},{64,96},{96,64},{128,160},{160,128},{192,224},{224,1... | collective-permute-start | bytes 172040 | tf_op jit(solution)/shard_map/ppermute | solution.py:291
  78.3 8.7 %all-to-all-start.2 = ((bf16[4,8,1792]{2,1,0:T(8,128)(2,1)}), bf16[4,8,1792]{2,1,0:T(8,128)(2,1)S(1)}, u32[]{:S(2)}, u32[]{:S(2)}) async-start(bf16[4,8,1792]{2,1,0:T(8,128)(2,1)} %both_cores.1), calls=%async_computation.2 | async-start | bytes 229376 | tf_op jit(solution)/shard_map/all_to_all | solution.py:301
